TPU v7x, 32 devices: a whole 2x2x4 slice. The times are simulated.
32 devices in a mesh: orb: 8 (over y, x, core), walk: 4 (over z).
Axes of the slice: x: 2, y: 2, z: 4, core: 2. Of those that a mesh axis runs over, the one named last changes fastest.
Arguments:
- chol: bfloat16 [32, 2048, 2048], P(None, 'orb', 'walk'), may hold values from -6 to 6
- orbitals: bfloat16 [2048, 1024], replicated, may hold values from -0.125 to 0.125
- greens: bfloat16 [4, 1024, 2048], P('walk'), may hold values from -0.00390625 to 0.00390625
- shift: float32 [32], P('orb'), may hold values from -6 to 6
Outputs:
- force_bias: float32 [4, 32], P('walk', 'orb')
- rotated: bfloat16 [32, 1024, 2048], P('orb', None, 'walk')
All inputs are finite; a program needn't handle non-finite values.
Results may differ from a plain program's by a relative error of at most 0.007.
Values may be sent and summed in bfloat16 or wider, within the bound.
No kernel may reach another device: no remote copies, remote signals or barrier semaphores. Data moves between devices by JAX's collectives and lax.ppermute only.
A program may use at most 64 MiB of HBM per device.

v0:
```python
import functools

import jax
import jax.numpy as jnp
from jax import lax
from jax.experimental import pallas as pl
from jax.experimental.pallas import tpu as pltpu
from jax.sharding import PartitionSpec as P


MIB = 2**20


def tied(value, *after):
    return lax.optimization_barrier((value, *after))[0]


def in_hbm(value):
    return pltpu.with_memory_space_constraint(value, pltpu.HBM)


def params(mib):
    return pltpu.CompilerParams(vmem_limit_bytes=mib * MIB)


def offsets(owners):
    chips = lambda k: (k >> 1).bit_count()
    first = [k for k in range(owners - 2, 0, -2) if chips(k) == 1]
    second = [k + 1 for k in first] + [1]
    return first, second, [k for k in range(1, owners) if chips(k) > 1]


def last_parts(columns):
    return 2 if columns % 256 == 0 else 1


def cost(flops, moved):
    return pl.CostEstimate(flops=flops, bytes_accessed=moved, transcendentals=0)


def first_kernel(offsets, count, chol_ref, *refs):
    out_refs, sems = refs[:-1], refs[-1]
    me = lax.axis_index("orb")
    copies = []
    for n, (k, out_ref) in enumerate(zip(offsets, out_refs)):
        piece = chol_ref.at[pl.ds((me ^ k) * count, out_ref.shape[0])]
        copies.append(pltpu.make_async_copy(piece, out_ref, sems.at[n]))
        copies[-1].start()
    for copy in copies:
        copy.wait()


def first_pieces(chol, offsets, count, size):
    shape = jax.ShapeDtypeStruct((size,) + chol.shape[1:], chol.dtype)
    return pl.pallas_call(
        functools.partial(first_kernel, offsets, count),
        out_shape=[shape] * len(offsets),
        in_specs=[pl.BlockSpec(memory_space=pl.ANY)],
        out_specs=[pl.BlockSpec(memory_space=pltpu.VMEM)] * len(offsets),
        scratch_shapes=[pltpu.SemaphoreType.DMA((len(offsets),))],
        compiler_params=params(8),
        cost_estimate=cost(2**20, 4 * len(offsets) * size * chol[0].size),
        name="first",
    )(in_hbm(chol))


def terms_kernel(place, chol_ref, *refs):
    product_refs, out_ref = refs[:-1], refs[-1]
    for v in range(chol_ref.shape[0]):
        block = chol_ref[v].astype(jnp.float32)
        for w, product in enumerate(product_refs):
            terms = jnp.sum(product[...].astype(jnp.float32) * block, axis=0, keepdims=True)
            out_ref[w, v] = terms


def force_terms(chol, products, me, count):
    vectors, rows, columns = chol.shape
    walkers = len(products)
    whole = pl.BlockSpec((rows, columns), lambda v, place: (0, 0))
    return pl.pallas_call(
        terms_kernel,
        out_shape=jax.ShapeDtypeStruct((walkers, vectors, 1, columns), jnp.float32),
        grid_spec=pltpu.PrefetchScalarGridSpec(
            num_scalar_prefetch=1,
            grid=(vectors // count,),
            in_specs=[pl.BlockSpec((count, rows, columns), lambda v, place: (place[0] ^ v, 0, 0))]
            + [whole] * walkers,
            out_specs=pl.BlockSpec((walkers, count, 1, columns), lambda v, place: (0, v, 0, 0)),
        ),
        compiler_params=params(12),
        cost_estimate=cost(2 * walkers * chol.size, 2 * chol.size),
        name="terms",
    )(me, in_hbm(chol), *products)


def turn_kernel(place, source_ref, out_ref):
    out_ref[...] = source_ref[...].T


def turned(orbitals, owners, rows):
    occupied = orbitals.shape[1]
    blocks = owners.shape[0]
    return pl.pallas_call(
        turn_kernel,
        out_shape=jax.ShapeDtypeStruct((occupied, blocks * rows), orbitals.dtype),
        grid_spec=pltpu.PrefetchScalarGridSpec(
            num_scalar_prefetch=1,
            grid=(blocks,),
            in_specs=[pl.BlockSpec((rows, occupied), lambda k, place: (place[k], 0))],
            out_specs=pl.BlockSpec((occupied, rows), lambda k, place: (0, k)),
        ),
        compiler_params=params(8),
        cost_estimate=cost(blocks * rows * occupied * 300, 4 * blocks * rows * occupied),
        name="turn",
    )(owners, orbitals)


def near_kernel(counts, lhs_ref, *refs):
    piece_refs, out_ref, rhs = refs[:-2], refs[-2], refs[-1]
    rows = piece_refs[0].shape[1]
    vector = pl.program_id(0)
    piece_refs = iter(piece_refs)
    for k, pieces in enumerate(counts):
        at, start = pl.ds(k * rows, rows), 0
        for size in pieces:
            piece = next(piece_refs)

            @pl.when((vector >= start) & (vector < start + size))
            def _():
                rhs[at, :] = piece[0]

            start += size
    out_ref[0] = jnp.dot(lhs_ref[...], rhs[...], preferred_element_type=jnp.float32)


def near_sum(lhs, blocks):
    counts = [[piece.shape[0] for piece in pieces] for pieces in blocks]
    count, (_, rows, columns) = sum(counts[0]), blocks[0][0].shape
    occupied, depth = lhs.shape
    specs = [pl.BlockSpec((occupied, depth), lambda g: (0, 0))]
    for pieces in counts:
        start = 0
        for size in pieces:
            at = functools.partial(lambda start, size, g: (jnp.clip(g - start, 0, size - 1), 0, 0), start, size)
            specs.append(pl.BlockSpec((1, rows, columns), at))
            start += size
    return pl.pallas_call(
        functools.partial(near_kernel, counts),
        out_shape=jax.ShapeDtypeStruct((count, occupied, columns), jnp.float32),
        grid=(count,),
        in_specs=specs,
        out_specs=pl.BlockSpec((1, occupied, columns), lambda g: (g, 0, 0)),
        scratch_shapes=[pltpu.VMEM((depth, columns), jnp.bfloat16)],
        compiler_params=params(24),
        cost_estimate=cost(2 * count * occupied * depth * columns, 4 * count * occupied * columns),
        name="near",
    )(in_hbm(lhs), *(in_hbm(piece) for pieces in blocks for piece in pieces))


def far_kernel(first, blocks, lhs_ref, near_ref, *refs):
    block_refs, (out_ref, rhs, held, sems) = refs[:blocks], refs[-4:]
    size, rows, _ = block_refs[0].shape
    tiles = sems.shape[1]
    tile = held.shape[1] // tiles
    copies = []
    for v in range(size):
        for k, block in enumerate(block_refs):
            rhs[v, k * rows : (k + 1) * rows, :] = block[v]
        for t in range(tiles):
            part = pl.ds(t * tile, tile)
            total = near_ref[first + v, part, :] + jnp.dot(
                lhs_ref[part, :], rhs[v], preferred_element_type=jnp.float32
            )
            held[v, part, :] = total.astype(held.dtype)
            copy = pltpu.make_async_copy(
                held.at[v, part, :], out_ref.at[first + v, part, :], sems.at[v, t]
            )
            copy.start()
            copies.append(copy)
    for copy in copies:
        copy.wait()


def far_sum(lhs, near, blocks, rotated, first):
    size, _, columns = blocks[0].shape
    occupied, depth = lhs.shape
    tiles = 4
    given = [] if rotated is None else [rotated]
    whole, left = pl.BlockSpec(memory_space=pltpu.VMEM), pl.BlockSpec(memory_space=pl.ANY)
    return pl.pallas_call(
        functools.partial(far_kernel, first, len(blocks)),
        out_shape=jax.ShapeDtypeStruct(near.shape, jnp.bfloat16),
        in_specs=[whole] * (2 + len(blocks)) + [left] * len(given),
        out_specs=left,
        scratch_shapes=[
            pltpu.VMEM((size, depth, columns), jnp.bfloat16),
            pltpu.VMEM((size, occupied, columns), jnp.bfloat16),
            pltpu.SemaphoreType.DMA((size, tiles)),
        ],
        input_output_aliases={2 + len(blocks): 0} if given else {},
        compiler_params=params(20),
        cost_estimate=cost(2 * size * occupied * depth * columns, 4 * size * occupied * columns),
        name="far",
    )(lhs, near, *blocks, *given)


def middle_kernel(vector, lhs_ref, near_ref, *refs):
    block_refs, out_ref = refs[:-1], refs[-1]
    rows = block_refs[0].shape[1]
    tile = out_ref.shape[0] // 4
    for t in range(4):
        at = pl.ds(t * tile, tile)
        total = near_ref[vector, at, :]
        for k, block in enumerate(block_refs):
            total += jnp.dot(
                lhs_ref[at, k * rows : (k + 1) * rows], block[0], preferred_element_type=jnp.float32
            )
        out_ref[at, :] = total


def middle_sum(lhs, near, blocks, vector):
    _, rows, columns = blocks[0].shape
    occupied = lhs.shape[0]
    return pl.pallas_call(
        functools.partial(middle_kernel, vector),
        out_shape=jax.ShapeDtypeStruct((occupied, columns), jnp.float32),
        in_specs=[pl.BlockSpec(memory_space=pltpu.VMEM)] * (2 + len(blocks)),
        out_specs=pl.BlockSpec(memory_space=pltpu.VMEM),
        compiler_params=params(16),
        cost_estimate=cost(2 * occupied * rows * columns * len(blocks), 8 * occupied * columns),
        name="middle",
    )(lhs, near, *blocks)


def last_kernel(vector, start, lhs_ref, near_ref, block_ref, _, out_ref, held, sems):
    _, rows, columns = block_ref.shape
    at_columns, weights = pl.ds(start, columns), pl.ds(lhs_ref.shape[1] - rows, rows)
    tiles = sems.shape[0]
    tile = held.shape[0] // tiles
    copies = []
    for t in range(tiles):
        at = pl.ds(t * tile, tile)
        total = near_ref[at, at_columns] + jnp.dot(
            lhs_ref[at, weights], block_ref[0], preferred_element_type=jnp.float32
        )
        held[at, :] = total.astype(held.dtype)
        copies.append(
            pltpu.make_async_copy(held.at[at, :], out_ref.at[vector, at, at_columns], sems.at[t])
        )
        copies[-1].start()
    for copy in copies:
        copy.wait()


def last_sum(lhs, near, block, rotated, vector, start):
    _, rows, columns = block.shape
    occupied, tiles = lhs.shape[0], 8
    whole, left = pl.BlockSpec(memory_space=pltpu.VMEM), pl.BlockSpec(memory_space=pl.ANY)
    return pl.pallas_call(
        functools.partial(last_kernel, vector, start),
        out_shape=jax.ShapeDtypeStruct(rotated.shape, rotated.dtype),
        in_specs=[whole, whole, whole, left],
        out_specs=left,
        scratch_shapes=[
            pltpu.VMEM((occupied, columns), rotated.dtype),
            pltpu.SemaphoreType.DMA((tiles,)),
        ],
        input_output_aliases={3: 0},
        compiler_params=params(16),
        cost_estimate=cost(2 * occupied * rows * columns, 4 * occupied * columns),
        name="last",
    )(lhs, near, block, rotated)


def local(owners, chol, orbitals, greens, shift):
    walkers = greens.shape[2] // chol.shape[2]
    count = chol.shape[0] // owners
    rows, columns = chol.shape[1:]
    me, mine = lax.axis_index("orb"), lax.axis_index("walk")
    first, second, far_offsets = offsets(owners)

    def swap(value, axis, k, size):
        return lax.ppermute(value, axis, [(i, i ^ k) for i in range(size)])

    def part(source, k, start=0, stop=count):
        return lax.dynamic_slice_in_dim(source, (me ^ k) * count + start, stop - start, 0)

    source, near = chol, {k: [] for k in first}
    for start, stop in ((0, 1), (1, count)):
        if start == 0:
            pieces = first_pieces(chol, first, count, stop)
        else:
            pieces = [part(source, k, start, stop) for k in first]
        source, orbitals, greens = tied((source, orbitals, greens), *pieces)
        for k, piece in zip(first, pieces):
            near[k].append(swap(piece, "orb", k, owners))

    pieces = {k: part(source, k) for k in [0] + second}
    source = tied(source, *pieces.values())
    near[0] = [pieces[0]]
    for k in second:
        near[k] = [swap(pieces[k], "orb", k, owners)]

    arrived = [near[k][0] for k in first]
    orbitals, greens = tied((orbitals, greens), *pieces.values(), *arrived)
    orbital_rows = lax.dynamic_slice_in_dim(orbitals, me * rows, rows, 0)
    products = jnp.dot(orbital_rows, greens[0], preferred_element_type=jnp.float32)
    products = products.astype(jnp.bfloat16)
    pieces = [
        lax.dynamic_slice_in_dim(products, (mine ^ k) * columns, columns, 1) for k in range(walkers)
    ]
    source = tied(source, *pieces)
    arrived = pieces[:1] + [swap(pieces[k], "walk", k, walkers) for k in range(1, walkers)]

    cuts = [(a, b) for a, b in ((0, count - 2), (count - 2, count - 1)) if a < b]
    far = []
    for span in cuts:
        pieces = [part(source, k, *span) for k in far_offsets]
        source = tied(source, *pieces)
        far.append([swap(piece, "orb", k, owners) for k, piece in zip(far_offsets, pieces)])

    order = [0] + first + second
    lhs_near = turned(orbitals, jnp.array(order, jnp.int32) ^ me, rows)
    lhs_far = turned(orbitals, jnp.array(far_offsets, jnp.int32) ^ me, rows)

    terms = force_terms(chol, arrived, jnp.stack([me, mine]).astype(jnp.int32), count)
    terms = terms.sum(axis=(2, 3))
    total = terms[0] + sum(swap(terms[k], "walk", k, walkers) for k in range(1, walkers))
    total = total.reshape(owners, count)
    even = total[0::2] + swap(total[1::2], "orb", 1, owners)
    sums = [swap(even[k : k + 1], "orb", 2 * k, owners) for k in range(1, owners // 2)]

    source = tied(source, even)
    pieces = [part(source, k, count - 1) for k in far_offsets]
    middle = [swap(piece, "orb", k, owners) for k, piece in zip(far_offsets[:-1], pieces)]
    half = columns // last_parts(columns)
    last = [
        swap(pieces[-1][..., at : at + half], "orb", far_offsets[-1], owners)
        for at in range(0, columns, half)
    ]

    partial = near_sum(lhs_near, [near[k] for k in order])
    sums = tied(sums, partial)
    force_bias = even[:1] + sum(sums) - shift[None, :]
    rotated = None
    for (start, _), blocks in zip(cuts, far):
        rotated = far_sum(lhs_far, partial, blocks, rotated, start)
    partial = middle_sum(lhs_far, partial, middle, count - 1)
    for n, block in enumerate(last):
        rotated = last_sum(lhs_far, partial, block, rotated, count - 1, n * half)
    return force_bias, rotated


def solution(mesh):
    in_specs = (P(None, "orb", "walk"), P(), P("walk", None, None), P("orb"))
    out_specs = (P("walk", "orb"), P("orb", None, "walk"))
    owners = mesh.shape["orb"]

    def step(chol, *args):
        def body(*args):
            return local(owners, *args)

        run = jax.shard_map(
            body, mesh=mesh, in_specs=in_specs, out_specs=out_specs, check_vma=False
        )
        return run(chol, *args)

    return step
```

profile of v0, /device:TPU:0, one launch (start us, length us, event | category | flops | bytes accessed | tf_op | source)
XLA Modules:
  0.0 147.9 jit_solution(4766415499700334782)
XLA Ops:
  1.7 3.1 %collective-permute-start = (bf16[1,256,512]{2,1,0:T(8,128)(2,1)S(1)}, bf16[1,256,512]{2,1,0:T(8,128)(2,1)S(1)}, u32[]{:S(2)}, u32[]{:S(2)}) collective-permute-start(bf16[1,256,512]{2,1,0:T(8,128)(2,1)S(1)} %get-tuple-element.20), channel_id=1, source_target_pairs={{0,16},{4,20},{8,24},{12,28},{16,0},{20,4},{24,8},{28,12},{1,17},{... | collective-permute-start | bytes 786440 | tf_op jit(solution)/shard_map/ppermute | solution.py:283
  4.8 1.5 %collective-permute-start.1 = (bf16[1,256,512]{2,1,0:T(8,128)(2,1)S(1)}, bf16[1,256,512]{2,1,0:T(8,128)(2,1)S(1)}, u32[]{:S(2)}, u32[]{:S(2)}) collective-permute-start(bf16[1,256,512]{2,1,0:T(8,128)(2,1)S(1)} %get-tuple-element.21), channel_id=1, source_target_pairs={{0,8},{4,12},{8,0},{12,4},{16,24},{20,28},{24,16},{28,20},{1,9},{5... | collective-permute-start | bytes 786440 | tf_op jit(solution)/shard_map/ppermute | solution.py:283
  6.2 2.7 %constant_dynamic-slice_fusion.15 = (bf16[3,256,512]{2,1,0:T(8,128)(2,1)}, bf16[3,256,512]{2,1,0:T(8,128)(2,1)}) fusion(bf16[32,256,512]{2,1,0:T(8,128)(2,1)} %chol_ref.3, s32[]{:T(128)S(6)} %select_n.52, s32[]{:T(128)S(6)} %select_n.51), kind=kLoop, calls=%fused_computation.20 | loop fusion | bytes 3145736 | tf_op jit(solution)/shard_map/dynamic_slice | solution.py:286
  9.0 3.9 %constant_dynamic-slice_fusion.11 = (bf16[4,256,512]{2,1,0:T(8,128)(2,1)S(1)}, bf16[4,256,512]{2,1,0:T(8,128)(2,1)S(1)}, bf16[4,256,512]{2,1,0:T(8,128)(2,1)}, bf16[4,256,512]{2,1,0:T(8,128)(2,1)}) fusion(bf16[32,256,512]{2,1,0:T(8,128)(2,1)} %chol_ref.3, s32[]{:T(128)S(6)} %select_n.56, s32[]{:T(128)S(6)} %select_n.55, s32[]{:T(128)S(6)} %select_n.54, ...), kind=kLoop, calls=%fused_computation.16 | loop fusion | bytes 8388624 | tf_op jit(solution)/shard_map/dynamic_slice | solution.py:286
  13.3 3.8 %fusion.2 = bf16[256,2048]{1,0:T(8,128)(2,1)S(1)} fusion(bf16[1,1024,2048]{2,1,0:T(8,128)(2,1)} %param.8, bf16[2048,1024]{1,0:T(8,128)(2,1)} %source_ref.1, s32[]{:T(128)S(6)} %select_n.57), kind=kOutput, calls=%fused_computation.2 | convolution fusion | flops 1074266112 | bytes 5767172 | tf_op jit(solution)/shard_map/dot_general | solution.py:307
  18.0 2.0 %collective-permute-start.2 = (bf16[256,512]{1,0:T(8,128)(2,1)}, bf16[256,512]{1,0:T(8,128)(2,1)S(1)}, u32[]{:S(2)}, u32[]{:S(2)}) collective-permute-start(bf16[256,512]{1,0:T(8,128)(2,1)} %get-tuple-element.52), channel_id=1, source_target_pairs={{0,1},{1,0},{2,3},{3,2},{4,5},{5,4},{6,7},{7,6},{8,9},{9,8},{10,11... | collective-permute-start | bytes 786440 | tf_op jit(solution)/shard_map/ppermute | solution.py:283
  20.0 2.6 %collective-permute-start.3 = (bf16[256,512]{1,0:T(8,128)(2,1)}, bf16[256,512]{1,0:T(8,128)(2,1)S(1)}, u32[]{:S(2)}, u32[]{:S(2)}) collective-permute-start(bf16[256,512]{1,0:T(8,128)(2,1)} %get-tuple-element.51), channel_id=1, source_target_pairs={{0,2},{1,3},{2,0},{3,1},{4,6},{5,7},{6,4},{7,5},{8,10},{9,11},{10,... | collective-permute-start | bytes 786440 | tf_op jit(solution)/shard_map/ppermute | solution.py:283
  22.7 9.0 %collective-permute-done.2.refs_1_ = bf16[256,512]{1,0:T(8,128)(2,1)S(1)} collective-permute-done((bf16[256,512]{1,0:T(8,128)(2,1)}, bf16[256,512]{1,0:T(8,128)(2,1)S(1)}, u32[]{:S(2)}, u32[]{:S(2)}) %collective-permute-start.2) | collective-permute-done | bytes 262176 | tf_op jit(solution)/shard_map/ppermute | solution.py:283
  31.6 9.9 %collective-permute-done.3.refs_2_ = bf16[256,512]{1,0:T(8,128)(2,1)S(1)} collective-permute-done((bf16[256,512]{1,0:T(8,128)(2,1)}, bf16[256,512]{1,0:T(8,128)(2,1)S(1)}, u32[]{:S(2)}, u32[]{:S(2)}) %collective-permute-start.3) | collective-permute-done | bytes 262176 | tf_op jit(solution)/shard_map/ppermute | solution.py:283
  41.5 8.0 %terms.1 = f32[4,32,1,512]{3,2,1,0:T(1,128)S(1)} custom-call(s32[2]{0:T(128)S(1)} %pad_add_fusion.place, bf16[32,256,512]{2,1,0:T(8,128)(2,1)} %chol_ref.3, bf16[256,512]{1,0:T(8,128)(2,1)S(1)} %get-tuple-element.53.refs_0_, bf16[256,512]{1,0:T(8,128)(2,1)S(1)} %collective-permute-done.2.refs_1_, bf16[256,512]{1,0:T(8,128)(2,1)S(1)} %collective-permute-done.3.refs_2_, ...), custom_call_target="tpu_custom_call" | custom-call | flops 33554432 | bytes 8388608 | tf_op jit(solution)/shard_map/terms/pallas_call | solution.py:80
  50.0 4.9 %collective-permute-start.5 = (f32[32]{0:T(128)S(1)}, f32[32]{0:T(128)S(1)}, u32[]{:S(2)}, u32[]{:S(2)}) collective-permute-start(f32[32]{0:T(128)S(1)} %get-tuple-element.59), channel_id=1, source_target_pairs={{0,1},{1,0},{2,3},{3,2},{4,5},{5,4},{6,7},{7,6},{8,9},{9,8},{10,11... | collective-permute-start | bytes 392 | tf_op jit(solution)/shard_map/ppermute | solution.py:283
  56.5 2.5 %collective-permute-start.7 = (f32[32]{0:T(128)S(1)}, f32[32]{0:T(128)S(1)}, u32[]{:S(2)}, u32[]{:S(2)}) collective-permute-start(f32[32]{0:T(128)S(1)} %get-tuple-element.58), channel_id=1, source_target_pairs={{0,3},{1,2},{2,1},{3,0},{4,7},{5,6},{6,5},{7,4},{8,11},{9,10},{10,... | collective-permute-start | bytes 392 | tf_op jit(solution)/shard_map/ppermute | solution.py:283
  59.4 1.5 %collective-permute-start.12 = (bf16[3,256,512]{2,1,0:T(8,128)(2,1)}, bf16[3,256,512]{2,1,0:T(8,128)(2,1)S(1)}, u32[]{:S(2)}, u32[]{:S(2)}) collective-permute-start(bf16[3,256,512]{2,1,0:T(8,128)(2,1)} %get-tuple-element.49), channel_id=1, source_target_pairs={{0,16},{4,20},{8,24},{12,28},{16,0},{20,4},{24,8},{28,12},{1,17},{... | collective-permute-start | bytes 2359304 | tf_op jit(solution)/shard_map/ppermute | solution.py:283
  63.2 1.5 %collective-permute-start.10 = (f32[1,4]{1,0:T(1,128)S(1)}, f32[1,4]{1,0:T(1,128)S(1)}, u32[]{:S(2)}, u32[]{:S(2)}) collective-permute-start(f32[1,4]{1,0:T(1,128)S(1)} %get-tuple-element.55), channel_id=1, source_target_pairs={{0,16},{4,20},{8,24},{12,28},{16,0},{20,4},{24,8},{28,12},{1,17},{... | collective-permute-start | bytes 56 | tf_op jit(solution)/shard_map/ppermute | solution.py:283
  64.7 11.8 %collective-permute-done.10 = f32[1,4]{1,0:T(1,128)S(1)} collective-permute-done((f32[1,4]{1,0:T(1,128)S(1)}, f32[1,4]{1,0:T(1,128)S(1)}, u32[]{:S(2)}, u32[]{:S(2)}) %collective-permute-start.10) | collective-permute-done | bytes 48 | tf_op jit(solution)/shard_map/ppermute | solution.py:283
  77.7 3.2 %collective-permute-done.11 = f32[1,4]{1,0:T(1,128)S(1)} collective-permute-done((f32[1,4]{1,0:T(1,128)S(1)}, f32[1,4]{1,0:T(1,128)S(1)}, u32[]{:S(2)}, u32[]{:S(2)}) %collective-permute-start.11) | collective-permute-done | bytes 48 | tf_op jit(solution)/shard_map/ppermute | solution.py:283
  81.0 1.5 %collective-permute-start.9 = (f32[1,4]{1,0:T(1,128)S(1)}, f32[1,4]{1,0:T(1,128)S(1)}, u32[]{:S(2)}, u32[]{:S(2)}) collective-permute-start(f32[1,4]{1,0:T(1,128)S(1)} %get-tuple-element.56), channel_id=1, source_target_pairs={{0,8},{4,12},{8,0},{12,4},{16,24},{20,28},{24,16},{28,20},{1,9},{5... | collective-permute-start | bytes 56 | tf_op jit(solution)/shard_map/ppermute | solution.py:283
  82.5 2.1 %collective-permute-done.9 = f32[1,4]{1,0:T(1,128)S(1)} collective-permute-done((f32[1,4]{1,0:T(1,128)S(1)}, f32[1,4]{1,0:T(1,128)S(1)}, u32[]{:S(2)}, u32[]{:S(2)}) %collective-permute-start.9) | collective-permute-done | bytes 48 | tf_op jit(solution)/shard_map/ppermute | solution.py:283
  84.6 1.5 %collective-permute-start.13 = (bf16[3,256,512]{2,1,0:T(8,128)(2,1)}, bf16[3,256,512]{2,1,0:T(8,128)(2,1)}, u32[]{:S(2)}, u32[]{:S(2)}) collective-permute-start(bf16[3,256,512]{2,1,0:T(8,128)(2,1)} %get-tuple-element.48), channel_id=1, source_target_pairs={{0,8},{4,12},{8,0},{12,4},{16,24},{20,28},{24,16},{28,20},{1,9},{5... | collective-permute-start | bytes 2359304 | tf_op jit(solution)/shard_map/ppermute | solution.py:283
  86.1 1.3 constant_dynamic-slice_fusion.5
  88.4 2.2 %copy-done = bf16[2048,1024]{1,0:T(8,128)(2,1)S(1)} copy-done((bf16[2048,1024]{1,0:T(8,128)(2,1)S(1)}, bf16[2048,1024]{1,0:T(8,128)(2,1)}, u32[]{:S(2)}) %copy-start) | copy-done | bytes 4194328
  91.6 2.0 %turn.2.lhs_ref = bf16[1024,1536]{1,0:T(8,128)(2,1)S(1)} custom-call(s32[6]{0:T(128)S(1)} %broadcast_xor_fusion.1.place, bf16[2048,1024]{1,0:T(8,128)(2,1)S(1)} %copy-done), custom_call_target="tpu_custom_call" | custom-call | flops 471859200 | bytes 6291456 | tf_op jit(solution)/shard_map/turn/pallas_call | solution.py:103
  93.6 1.7 %copy-done.1 = bf16[1024,1536]{1,0:T(8,128)(2,1)} copy-done((bf16[1024,1536]{1,0:T(8,128)(2,1)}, bf16[1024,1536]{1,0:T(8,128)(2,1)S(1)}, u32[]{:S(2)}) %copy-start.1) | copy-done | bytes 3145752
  97.3 1.5 %collective-permute-start.22 = (bf16[2,256,512]{2,1,0:T(8,128)(2,1)S(1)}, bf16[2,256,512]{2,1,0:T(8,128)(2,1)S(1)}, u32[]{:S(2)}, u32[]{:S(2)}) collective-permute-start(bf16[2,256,512]{2,1,0:T(8,128)(2,1)S(1)} %get-tuple-element.43), channel_id=1, source_target_pairs={{0,24},{4,28},{8,16},{12,20},{16,8},{20,12},{24,0},{28,4},{1,25},{... | collective-permute-start | bytes 1572872 | tf_op jit(solution)/shard_map/ppermute | solution.py:283
  98.8 4.6 %collective-permute-done.13.refs_4_ = bf16[3,256,512]{2,1,0:T(8,128)(2,1)} collective-permute-done((bf16[3,256,512]{2,1,0:T(8,128)(2,1)}, bf16[3,256,512]{2,1,0:T(8,128)(2,1)}, u32[]{:S(2)}, u32[]{:S(2)}) %collective-permute-start.13) | collective-permute-done | bytes 786464 | tf_op jit(solution)/shard_map/ppermute | solution.py:283
  103.9 2.4 %collective-permute-start.21 = (bf16[1,256,512]{2,1,0:T(8,128)(2,1)S(1)}, bf16[1,256,512]{2,1,0:T(8,128)(2,1)S(1)}, u32[]{:S(2)}, u32[]{:S(2)}) collective-permute-start(bf16[1,256,512]{2,1,0:T(8,128)(2,1)S(1)} %get-tuple-element.40), channel_id=1, source_target_pairs={{0,28},{4,24},{8,20},{12,16},{16,12},{20,8},{24,4},{28,0},{1,29},{... | collective-permute-start | bytes 786440 | tf_op jit(solution)/shard_map/ppermute | solution.py:283
  106.3 2.3 %collective-permute-start.17 = (bf16[1,256,512]{2,1,0:T(8,128)(2,1)S(1)}, bf16[1,256,512]{2,1,0:T(8,128)(2,1)S(1)}, u32[]{:S(2)}, u32[]{:S(2)}) collective-permute-start(bf16[1,256,512]{2,1,0:T(8,128)(2,1)S(1)} %constant_dynamic-slice_fusion.2), channel_id=1, source_target_pairs={{0,24},{4,28},{8,16},{12,20},{16,8},{20,12},{24,0},{28,4},{1,25},{... | collective-permute-start | bytes 786440 | tf_op jit(solution)/shard_map/ppermute | solution.py:283
  108.6 10.5 %near.1.near_ref = f32[4,1024,512]{2,1,0:T(8,128)S(1)} custom-call(bf16[1024,1536]{1,0:T(8,128)(2,1)} %copy-done.1, bf16[4,256,512]{2,1,0:T(8,128)(2,1)} %get-tuple-element.47.refs_0_, bf16[1,256,512]{2,1,0:T(8,128)(2,1)} %copy-done.4, bf16[3,256,512]{2,1,0:T(8,128)(2,1)} %copy-done.3, bf16[1,256,512]{2,1,0:T(8,128)(2,1)} %copy-done.5, ...), custom_call_target="tpu_custom_call" | custom-call | flops 6442450944 | bytes 8388608 | tf_op jit(solution)/shard_map/near/pallas_call | solution.py:147
  119.1 19.4 %collective-permute-done.17.refs_0_ = bf16[1,256,512]{2,1,0:T(8,128)(2,1)S(1)} collective-permute-done((bf16[1,256,512]{2,1,0:T(8,128)(2,1)S(1)}, bf16[1,256,512]{2,1,0:T(8,128)(2,1)S(1)}, u32[]{:S(2)}, u32[]{:S(2)}) %collective-permute-start.17) | collective-permute-done | bytes 262176 | tf_op jit(solution)/shard_map/ppermute | solution.py:283
  139.0 2.7 %collective-permute-start.18 = (bf16[1,256,256]{2,1,0:T(8,128)(2,1)S(1)}, bf16[1,256,256]{2,1,0:T(8,128)(2,1)S(1)}, u32[]{:S(2)}, u32[]{:S(2)}) collective-permute-start(bf16[1,256,256]{2,1,0:T(8,128)(2,1)S(1)} %get-tuple-element.39), channel_id=1, source_target_pairs={{0,28},{4,24},{8,20},{12,16},{16,12},{20,8},{24,4},{28,0},{1,29},{... | collective-permute-start | bytes 393224 | tf_op jit(solution)/shard_map/ppermute | solution.py:283
  141.7 2.0 %far.2.refs_2_ = bf16[4,1024,512]{2,1,0:T(8,128)(2,1)} custom-call(bf16[1024,512]{1,0:T(8,128)(2,1)S(1)} %turn.3.lhs_ref, f32[4,1024,512]{2,1,0:T(8,128)S(1)} %near.1.near_ref, bf16[2,256,512]{2,1,0:T(8,128)(2,1)S(1)} %collective-permute-done.22.refs_0_, bf16[2,256,512]{2,1,0:T(8,128)(2,1)S(1)} %collective-permute-done.23.refs_1_), custom_call_target="tpu_custom_call" | custom-call | flops 1073741824 | bytes 4194304 | tf_op jit(solution)/shard_map/far/pallas_call | solution.py:190
  143.8 1.5 far.3._
  (62 shorter events, 16.1 us)
Async XLA Ops:
  1.7 11.6 %collective-permute-start = (bf16[1,256,512]{2,1,0:T(8,128)(2,1)S(1)}, bf16[1,256,512]{2,1,0:T(8,128)(2,1)S(1)}, u32[]{:S(2)}, u32[]{:S(2)}) collective-permute-start(bf16[1,256,512]{2,1,0:T(8,128)(2,1)S(1)} %get-tuple-element.20), channel_id=1, source_target_pairs={{0,16},{4,20},{8,24},{12,28},{16,0},{20,4},{24,8},{28,12},{1,17},{... | collective-permute-start | bytes 786440 | tf_op jit(solution)/shard_map/ppermute | solution.py:283
  4.8 8.5 %collective-permute-start.1 = (bf16[1,256,512]{2,1,0:T(8,128)(2,1)S(1)}, bf16[1,256,512]{2,1,0:T(8,128)(2,1)S(1)}, u32[]{:S(2)}, u32[]{:S(2)}) collective-permute-start(bf16[1,256,512]{2,1,0:T(8,128)(2,1)S(1)} %get-tuple-element.21), channel_id=1, source_target_pairs={{0,8},{4,12},{8,0},{12,4},{16,24},{20,28},{24,16},{28,20},{1,9},{5... | collective-permute-start | bytes 786440 | tf_op jit(solution)/shard_map/ppermute | solution.py:283
  12.9 90.4 %collective-permute-start.14 = (bf16[4,256,512]{2,1,0:T(8,128)(2,1)}, bf16[4,256,512]{2,1,0:T(8,128)(2,1)}, u32[]{:S(2)}, u32[]{:S(2)}) collective-permute-start(bf16[4,256,512]{2,1,0:T(8,128)(2,1)} %get-tuple-element.46), channel_id=1, source_target_pairs={{0,20},{4,16},{8,28},{12,24},{16,4},{20,0},{24,12},{28,8},{1,21},{... | collective-permute-start | bytes 3145736 | tf_op jit(solution)/shard_map/ppermute | solution.py:283
  12.9 91.0 %collective-permute-start.15 = (bf16[4,256,512]{2,1,0:T(8,128)(2,1)S(1)}, bf16[4,256,512]{2,1,0:T(8,128)(2,1)}, u32[]{:S(2)}, u32[]{:S(2)}) collective-permute-start(bf16[4,256,512]{2,1,0:T(8,128)(2,1)S(1)} %get-tuple-element.45), channel_id=1, source_target_pairs={{0,12},{4,8},{8,4},{12,0},{16,28},{20,24},{24,20},{28,16},{1,13},{... | collective-permute-start | bytes 3145736 | tf_op jit(solution)/shard_map/ppermute | solution.py:283
  13.3 4.7 %copy-start.4 = (bf16[1,256,512]{2,1,0:T(8,128)(2,1)}, bf16[1,256,512]{2,1,0:T(8,128)(2,1)S(1)}, u32[]{:S(2)}) copy-start(bf16[1,256,512]{2,1,0:T(8,128)(2,1)S(1)} %collective-permute-done.refs_1_) | copy-start | bytes 786436
  13.3 4.7 %copy-start.5 = (bf16[1,256,512]{2,1,0:T(8,128)(2,1)}, bf16[1,256,512]{2,1,0:T(8,128)(2,1)S(1)}, u32[]{:S(2)}) copy-start(bf16[1,256,512]{2,1,0:T(8,128)(2,1)S(1)} %collective-permute-done.1.refs_3_) | copy-start | bytes 786436
  13.3 9.4 %copy-start.7 = (s32[6]{0:T(128)S(1)}, s32[6]{0:T(128)}, u32[]{:S(2)}) copy-start(s32[6]{0:T(128)} %constant.48.clone) | copy-start | bytes 76
  18.0 13.6 %collective-permute-start.2 = (bf16[256,512]{1,0:T(8,128)(2,1)}, bf16[256,512]{1,0:T(8,128)(2,1)S(1)}, u32[]{:S(2)}, u32[]{:S(2)}) collective-permute-start(bf16[256,512]{1,0:T(8,128)(2,1)} %get-tuple-element.52), channel_id=1, source_target_pairs={{0,1},{1,0},{2,3},{3,2},{4,5},{5,4},{6,7},{7,6},{8,9},{9,8},{10,11... | collective-permute-start | bytes 786440 | tf_op jit(solution)/shard_map/ppermute | solution.py:283
  20.0 21.5 %collective-permute-start.3 = (bf16[256,512]{1,0:T(8,128)(2,1)}, bf16[256,512]{1,0:T(8,128)(2,1)S(1)}, u32[]{:S(2)}, u32[]{:S(2)}) collective-permute-start(bf16[256,512]{1,0:T(8,128)(2,1)} %get-tuple-element.51), channel_id=1, source_target_pairs={{0,2},{1,3},{2,0},{3,1},{4,6},{5,7},{6,4},{7,5},{8,10},{9,11},{10,... | collective-permute-start | bytes 786440 | tf_op jit(solution)/shard_map/ppermute | solution.py:283
  22.6 18.9 %collective-permute-start.4 = (bf16[256,512]{1,0:T(8,128)(2,1)S(1)}, bf16[256,512]{1,0:T(8,128)(2,1)S(1)}, u32[]{:S(2)}, u32[]{:S(2)}) collective-permute-start(bf16[256,512]{1,0:T(8,128)(2,1)S(1)} %get-tuple-element.50), channel_id=1, source_target_pairs={{0,3},{1,2},{2,1},{3,0},{4,7},{5,6},{6,5},{7,4},{8,11},{9,10},{10,... | collective-permute-start | bytes 786440 | tf_op jit(solution)/shard_map/ppermute | solution.py:283
  31.6 74.7 %collective-permute-start.16 = (bf16[4,256,512]{2,1,0:T(8,128)(2,1)S(1)}, bf16[4,256,512]{2,1,0:T(8,128)(2,1)}, u32[]{:S(2)}, u32[]{:S(2)}) collective-permute-start(bf16[4,256,512]{2,1,0:T(8,128)(2,1)S(1)} %get-tuple-element.44), channel_id=1, source_target_pairs={{0,4},{4,0},{8,12},{12,8},{16,20},{20,16},{24,28},{28,24},{1,5},{5... | collective-permute-start | bytes 3145736 | tf_op jit(solution)/shard_map/ppermute | solution.py:283
  41.5 44.5 %copy-start.6 = (s32[2]{0:T(128)S(1)}, s32[2]{0:T(128)}, u32[]{:S(2)}) copy-start(s32[2]{0:T(128)} %constant.49.clone) | copy-start | bytes 28
  50.0 6.5 %collective-permute-start.5 = (f32[32]{0:T(128)S(1)}, f32[32]{0:T(128)S(1)}, u32[]{:S(2)}, u32[]{:S(2)}) collective-permute-start(f32[32]{0:T(128)S(1)} %get-tuple-element.59), channel_id=1, source_target_pairs={{0,1},{1,0},{2,3},{3,2},{4,5},{5,4},{6,7},{7,6},{8,9},{9,8},{10,11... | collective-permute-start | bytes 392 | tf_op jit(solution)/shard_map/ppermute | solution.py:283
  54.9 4.5 %collective-permute-start.6 = (f32[32]{0:T(128)S(1)}, f32[32]{0:T(128)S(1)}, u32[]{:S(2)}, u32[]{:S(2)}) collective-permute-start(f32[32]{0:T(128)S(1)} %get-tuple-element.57), channel_id=1, source_target_pairs={{0,2},{1,3},{2,0},{3,1},{4,6},{5,7},{6,4},{7,5},{8,10},{9,11},{10,... | collective-permute-start | bytes 392 | tf_op jit(solution)/shard_map/ppermute | solution.py:283
  56.5 5.4 %collective-permute-start.7 = (f32[32]{0:T(128)S(1)}, f32[32]{0:T(128)S(1)}, u32[]{:S(2)}, u32[]{:S(2)}) collective-permute-start(f32[32]{0:T(128)S(1)} %get-tuple-element.58), channel_id=1, source_target_pairs={{0,3},{1,2},{2,1},{3,0},{4,7},{5,6},{6,5},{7,4},{8,11},{9,10},{10,... | collective-permute-start | bytes 392 | tf_op jit(solution)/shard_map/ppermute | solution.py:283
  59.4 37.8 %collective-permute-start.12 = (bf16[3,256,512]{2,1,0:T(8,128)(2,1)}, bf16[3,256,512]{2,1,0:T(8,128)(2,1)S(1)}, u32[]{:S(2)}, u32[]{:S(2)}) collective-permute-start(bf16[3,256,512]{2,1,0:T(8,128)(2,1)} %get-tuple-element.49), channel_id=1, source_target_pairs={{0,16},{4,20},{8,24},{12,28},{16,0},{20,4},{24,8},{28,12},{1,17},{... | collective-permute-start | bytes 2359304 | tf_op jit(solution)/shard_map/ppermute | solution.py:283
  62.0 1.2 collective-permute-start.8
  63.2 13.3 %collective-permute-start.10 = (f32[1,4]{1,0:T(1,128)S(1)}, f32[1,4]{1,0:T(1,128)S(1)}, u32[]{:S(2)}, u32[]{:S(2)}) collective-permute-start(f32[1,4]{1,0:T(1,128)S(1)} %get-tuple-element.55), channel_id=1, source_target_pairs={{0,16},{4,20},{8,24},{12,28},{16,0},{20,4},{24,8},{28,12},{1,17},{... | collective-permute-start | bytes 56 | tf_op jit(solution)/shard_map/ppermute | solution.py:283
  76.5 4.5 %collective-permute-start.11 = (f32[1,4]{1,0:T(1,128)S(1)}, f32[1,4]{1,0:T(1,128)S(1)}, u32[]{:S(2)}, u32[]{:S(2)}) collective-permute-start(f32[1,4]{1,0:T(1,128)S(1)} %get-tuple-element.54), channel_id=1, source_target_pairs={{0,24},{4,28},{8,16},{12,20},{16,8},{20,12},{24,0},{28,4},{1,25},{... | collective-permute-start | bytes 56 | tf_op jit(solution)/shard_map/ppermute | solution.py:283
  81.0 3.6 %collective-permute-start.9 = (f32[1,4]{1,0:T(1,128)S(1)}, f32[1,4]{1,0:T(1,128)S(1)}, u32[]{:S(2)}, u32[]{:S(2)}) collective-permute-start(f32[1,4]{1,0:T(1,128)S(1)} %get-tuple-element.56), channel_id=1, source_target_pairs={{0,8},{4,12},{8,0},{12,4},{16,24},{20,28},{24,16},{28,20},{1,9},{5... | collective-permute-start | bytes 56 | tf_op jit(solution)/shard_map/ppermute | solution.py:283
  84.6 18.8 %collective-permute-start.13 = (bf16[3,256,512]{2,1,0:T(8,128)(2,1)}, bf16[3,256,512]{2,1,0:T(8,128)(2,1)}, u32[]{:S(2)}, u32[]{:S(2)}) collective-permute-start(bf16[3,256,512]{2,1,0:T(8,128)(2,1)} %get-tuple-element.48), channel_id=1, source_target_pairs={{0,8},{4,12},{8,0},{12,4},{16,24},{20,28},{24,16},{28,20},{1,9},{5... | collective-permute-start | bytes 2359304 | tf_op jit(solution)/shard_map/ppermute | solution.py:283
  88.4 2.2 %copy-start = (bf16[2048,1024]{1,0:T(8,128)(2,1)S(1)}, bf16[2048,1024]{1,0:T(8,128)(2,1)}, u32[]{:S(2)}) copy-start(bf16[2048,1024]{1,0:T(8,128)(2,1)} %source_ref.1) | copy-start | bytes 12582916
  93.6 1.7 %copy-start.1 = (bf16[1024,1536]{1,0:T(8,128)(2,1)}, bf16[1024,1536]{1,0:T(8,128)(2,1)S(1)}, u32[]{:S(2)}) copy-start(bf16[1024,1536]{1,0:T(8,128)(2,1)S(1)} %turn.2.lhs_ref) | copy-start | bytes 9437188
  97.2 11.4 %copy-start.3 = (bf16[3,256,512]{2,1,0:T(8,128)(2,1)}, bf16[3,256,512]{2,1,0:T(8,128)(2,1)S(1)}, u32[]{:S(2)}) copy-start(bf16[3,256,512]{2,1,0:T(8,128)(2,1)S(1)} %collective-permute-done.12.refs_2_) | copy-start | bytes 2359300
  97.3 41.7 %collective-permute-start.22 = (bf16[2,256,512]{2,1,0:T(8,128)(2,1)S(1)}, bf16[2,256,512]{2,1,0:T(8,128)(2,1)S(1)}, u32[]{:S(2)}, u32[]{:S(2)}) collective-permute-start(bf16[2,256,512]{2,1,0:T(8,128)(2,1)S(1)} %get-tuple-element.43), channel_id=1, source_target_pairs={{0,24},{4,28},{8,16},{12,20},{16,8},{20,12},{24,0},{28,4},{1,25},{... | collective-permute-start | bytes 1572872 | tf_op jit(solution)/shard_map/ppermute | solution.py:283
  103.3 38.4 %collective-permute-start.23 = (bf16[2,256,512]{2,1,0:T(8,128)(2,1)S(1)}, bf16[2,256,512]{2,1,0:T(8,128)(2,1)S(1)}, u32[]{:S(2)}, u32[]{:S(2)}) collective-permute-start(bf16[2,256,512]{2,1,0:T(8,128)(2,1)S(1)} %get-tuple-element.42), channel_id=1, source_target_pairs={{0,28},{4,24},{8,20},{12,16},{16,12},{20,8},{24,4},{28,0},{1,29},{... | collective-permute-start | bytes 1572872 | tf_op jit(solution)/shard_map/ppermute | solution.py:283
  103.3 40.4 %collective-permute-start.20 = (bf16[1,256,512]{2,1,0:T(8,128)(2,1)S(1)}, bf16[1,256,512]{2,1,0:T(8,128)(2,1)S(1)}, u32[]{:S(2)}, u32[]{:S(2)}) collective-permute-start(bf16[1,256,512]{2,1,0:T(8,128)(2,1)S(1)} %get-tuple-element.41), channel_id=1, source_target_pairs={{0,24},{4,28},{8,16},{12,20},{16,8},{20,12},{24,0},{28,4},{1,25},{... | collective-permute-start | bytes 786440 | tf_op jit(solution)/shard_map/ppermute | solution.py:283
  103.9 39.8 %collective-permute-start.21 = (bf16[1,256,512]{2,1,0:T(8,128)(2,1)S(1)}, bf16[1,256,512]{2,1,0:T(8,128)(2,1)S(1)}, u32[]{:S(2)}, u32[]{:S(2)}) collective-permute-start(bf16[1,256,512]{2,1,0:T(8,128)(2,1)S(1)} %get-tuple-element.40), channel_id=1, source_target_pairs={{0,28},{4,24},{8,20},{12,16},{16,12},{20,8},{24,4},{28,0},{1,29},{... | collective-permute-start | bytes 786440 | tf_op jit(solution)/shard_map/ppermute | solution.py:283
  106.3 32.2 %collective-permute-start.17 = (bf16[1,256,512]{2,1,0:T(8,128)(2,1)S(1)}, bf16[1,256,512]{2,1,0:T(8,128)(2,1)S(1)}, u32[]{:S(2)}, u32[]{:S(2)}) collective-permute-start(bf16[1,256,512]{2,1,0:T(8,128)(2,1)S(1)} %constant_dynamic-slice_fusion.2), channel_id=1, source_target_pairs={{0,24},{4,28},{8,16},{12,20},{16,8},{20,12},{24,0},{28,4},{1,25},{... | collective-permute-start | bytes 786440 | tf_op jit(solution)/shard_map/ppermute | solution.py:283
  138.6 6.7 %collective-permute-start.19 = (bf16[1,256,256]{2,1,0:T(8,128)(2,1)S(1)}, bf16[1,256,256]{2,1,0:T(8,128)(2,1)S(1)}, u32[]{:S(2)}, u32[]{:S(2)}) collective-permute-start(bf16[1,256,256]{2,1,0:T(8,128)(2,1)S(1)} %get-tuple-element.38), channel_id=1, source_target_pairs={{0,28},{4,24},{8,20},{12,16},{16,12},{20,8},{24,4},{28,0},{1,29},{... | collective-permute-start | bytes 393224 | tf_op jit(solution)/shard_map/ppermute | solution.py:283
  139.0 7.9 %collective-permute-start.18 = (bf16[1,256,256]{2,1,0:T(8,128)(2,1)S(1)}, bf16[1,256,256]{2,1,0:T(8,128)(2,1)S(1)}, u32[]{:S(2)}, u32[]{:S(2)}) collective-permute-start(bf16[1,256,256]{2,1,0:T(8,128)(2,1)S(1)} %get-tuple-element.39), channel_id=1, source_target_pairs={{0,28},{4,24},{8,20},{12,16},{16,12},{20,8},{24,4},{28,0},{1,29},{... | collective-permute-start | bytes 393224 | tf_op jit(solution)/shard_map/ppermute | solution.py:283
  145.2 1.1 copy-start.2
where the time goes:
time: 148 us
  waiting for transfers between devices  63 us (43%)
  starting transfers between devices  34.8 us (24%)
  Pallas kernels  28.6 us (19%)
  local copies, waits for them, and re-layouts  15.9 us (11%)
  matrix products  3.79 us (3%)
    ppermute x24, waiting for transfers between devices, swap(): return lax.ppermute(value, axis, [(i, i ^ k) for i in range(size)])  63 us
    ppermute x24, starting transfers between devices, swap(): return lax.ppermute(value, axis, [(i, i ^ k) for i in range(size)])  34.8 us
    pallas_call x1, Pallas kernels, near_sum(): pl.pallas_call(functools.partial(near_kernel, counts), out_shape=jax.Shap...  10.5 us
    dynamic_slice x5, local copies, waits for them, and re-layouts, part(): lax.dynamic_slice_in_dim(source, (me ^ k) * count + start, stop - start, 0)  9.98 us
    pallas_call x1, Pallas kernels, force_terms(): pl.pallas_call(terms_kernel, out_shape=jax.ShapeDtypeStruct((walkers, vec...  8.04 us
    unnamed x16, local copies, waits for them, and re-layouts  3.87 us
    dot_general x1, matrix products, local(): jnp.dot(orbital_rows, greens[0], preferred_element_type=jnp.float32)  3.79 us
    pallas_call x2, Pallas kernels, far_sum(): pl.pallas_call(functools.partial(far_kernel, first, len(blocks)), out_sha...  3.49 us
  transfers between devices with their start and end apart: 24, of which 11 were waited for; matrix products, arithmetic and copies ran while one was open for 11% of the time, Pallas kernels for 18%

commit v1 on v0

--- a/solution.py
+++ b/solution.py
@@ -157,8 +157,8 @@
     )(in_hbm(lhs), *(in_hbm(piece) for pieces in blocks for piece in pieces))
 
 
-def far_kernel(first, blocks, lhs_ref, near_ref, *refs):
-    block_refs, (out_ref, rhs, held, sems) = refs[:blocks], refs[-4:]
+def far_kernel(lhs_ref, near_ref, *refs):
+    block_refs, (out_ref, rhs, held, sems) = refs[:-4], refs[-4:]
     size, rows, _ = block_refs[0].shape
     tiles = sems.shape[1]
     tile = held.shape[1] // tiles
@@ -167,41 +167,35 @@
         for k, block in enumerate(block_refs):
             rhs[v, k * rows : (k + 1) * rows, :] = block[v]
         for t in range(tiles):
-            part = pl.ds(t * tile, tile)
-            total = near_ref[first + v, part, :] + jnp.dot(
-                lhs_ref[part, :], rhs[v], preferred_element_type=jnp.float32
+            at = pl.ds(t * tile, tile)
+            total = near_ref[v, at, :] + jnp.dot(
+                lhs_ref[at, :], rhs[v], preferred_element_type=jnp.float32
             )
-            held[v, part, :] = total.astype(held.dtype)
-            copy = pltpu.make_async_copy(
-                held.at[v, part, :], out_ref.at[first + v, part, :], sems.at[v, t]
-            )
-            copy.start()
-            copies.append(copy)
+            held[v, at, :] = total.astype(held.dtype)
+            copies.append(pltpu.make_async_copy(held.at[v, at, :], out_ref.at[v, at, :], sems.at[v, t]))
+            copies[-1].start()
     for copy in copies:
         copy.wait()
 
 
-def far_sum(lhs, near, blocks, rotated, first):
+def far_sum(lhs, near, blocks):
     size, _, columns = blocks[0].shape
     occupied, depth = lhs.shape
     tiles = 4
-    given = [] if rotated is None else [rotated]
-    whole, left = pl.BlockSpec(memory_space=pltpu.VMEM), pl.BlockSpec(memory_space=pl.ANY)
-    return pl.pallas_call(
-        functools.partial(far_kernel, first, len(blocks)),
+    return pl.pallas_call(
+        far_kernel,
         out_shape=jax.ShapeDtypeStruct(near.shape, jnp.bfloat16),
-        in_specs=[whole] * (2 + len(blocks)) + [left] * len(given),
-        out_specs=left,
+        in_specs=[pl.BlockSpec(memory_space=pltpu.VMEM)] * (2 + len(blocks)),
+        out_specs=pl.BlockSpec(memory_space=pl.ANY),
         scratch_shapes=[
             pltpu.VMEM((size, depth, columns), jnp.bfloat16),
             pltpu.VMEM((size, occupied, columns), jnp.bfloat16),
             pltpu.SemaphoreType.DMA((size, tiles)),
         ],
-        input_output_aliases={2 + len(blocks): 0} if given else {},
         compiler_params=params(20),
         cost_estimate=cost(2 * size * occupied * depth * columns, 4 * size * occupied * columns),
         name="far",
-    )(lhs, near, *blocks, *given)
+    )(lhs, near, *blocks)
 
 
 def middle_kernel(vector, lhs_ref, near_ref, *refs):
@@ -312,12 +306,9 @@
     source = tied(source, *pieces)
     arrived = pieces[:1] + [swap(pieces[k], "walk", k, walkers) for k in range(1, walkers)]
 
-    cuts = [(a, b) for a, b in ((0, count - 2), (count - 2, count - 1)) if a < b]
-    far = []
-    for span in cuts:
-        pieces = [part(source, k, *span) for k in far_offsets]
-        source = tied(source, *pieces)
-        far.append([swap(piece, "orb", k, owners) for k, piece in zip(far_offsets, pieces)])
+    pieces = [part(source, k, 0, count - 1) for k in far_offsets]
+    source = tied(source, *pieces)
+    far = [swap(piece, "orb", k, owners) for k, piece in zip(far_offsets, pieces)]
 
     order = [0] + first + second
     lhs_near = turned(orbitals, jnp.array(order, jnp.int32) ^ me, rows)
@@ -342,9 +333,7 @@
     partial = near_sum(lhs_near, [near[k] for k in order])
     sums = tied(sums, partial)
     force_bias = even[:1] + sum(sums) - shift[None, :]
-    rotated = None
-    for (start, _), blocks in zip(cuts, far):
-        rotated = far_sum(lhs_far, partial, blocks, rotated, start)
+    rotated = far_sum(lhs_far, partial, far)
     partial = middle_sum(lhs_far, partial, middle, count - 1)
     for n, block in enumerate(last):
         rotated = last_sum(lhs_far, partial, block, rotated, count - 1, n * half)

time: 148 us -> 142 us (0.959)
  starting transfers between devices: 34.8 us -> 21.9 us
  waiting for transfers between devices: 63 us -> 70.3 us
  local copies, waits for them, and re-layouts: 15.9 us -> 17.6 us
  Pallas kernels: 28.6 us -> 27 us
    ppermute x24 -> x22, starting transfers between devices: 34.8 us -> 21.9 us  [swap(): return lax.ppermute(value, axis, [(i, i ^ k) for i in range(size)])]
    ppermute x24 -> x22, waiting for transfers between devices: 63 us -> 70.3 us  [swap(): return lax.ppermute(value, axis, [(i, i ^ k) for i in range(size)])]
    unnamed x16 -> x18, local copies, waits for them, and re-layouts: 3.87 us -> 5.02 us
    pallas_call x2 -> x1, Pallas kernels: 3.49 us -> 2.61 us  [far_sum(): pl.pallas_call(far_kernel, out_shape=jax.ShapeDtypeStruct(near.shape, jnp...]
    dynamic_slice x5 -> x4, local copies, waits for them, and re-layouts: 9.98 us -> 10.5 us  [part(): lax.dynamic_slice_in_dim(source, (me ^ k) * count + start, stop - start, 0)]
  transfers between devices with their start and end apart: 24 -> 22, of which waited for: 11 -> 11; matrix products, arithmetic and copies ran while one was open for 11% -> 9% of each run, Pallas kernels for 18% -> 18%
where the time goes in v1:
time: 142 us; the launch traced here: 141 us
  waiting for transfers between devices  70.3 us (50%)
  Pallas kernels  27 us (19%)
  starting transfers between devices  21.9 us (15%)
  local copies, waits for them, and re-layouts  17.6 us (12%)
  matrix products  2.47 us (2%)
    ppermute x22, waiting for transfers between devices, swap(): return lax.ppermute(value, axis, [(i, i ^ k) for i in range(size)])  70.3 us
    ppermute x22, starting transfers between devices, swap(): return lax.ppermute(value, axis, [(i, i ^ k) for i in range(size)])  21.9 us
    dynamic_slice x4, local copies, waits for them, and re-layouts, part(): lax.dynamic_slice_in_dim(source, (me ^ k) * count + start, stop - start, 0)  10.5 us
    pallas_call x1, Pallas kernels, near_sum(): pl.pallas_call(functools.partial(near_kernel, counts), out_shape=jax.Shap...  10.5 us
    pallas_call x1, Pallas kernels, force_terms(): pl.pallas_call(terms_kernel, out_shape=jax.ShapeDtypeStruct((walkers, vec...  7.33 us
    unnamed x18, local copies, waits for them, and re-layouts  5.02 us
    pallas_call x2, Pallas kernels, turned(): pl.pallas_call(turn_kernel, out_shape=jax.ShapeDtypeStruct((occupied, blo...  2.99 us
  transfers between devices with their start and end apart: 22, of which 11 were waited for; matrix products, arithmetic and copies ran while one was open for 9% of the time, Pallas kernels for 18%

profile of v1, /device:TPU:0, one launch (start us, length us, event | category | flops | bytes accessed | tf_op | source)
XLA Modules:
  0.0 141.1 jit_solution(3500860312498746195)
XLA Ops:
  0.6 1.1 first.1
  1.7 3.1 %collective-permute-start = (bf16[1,256,512]{2,1,0:T(8,128)(2,1)S(1)}, bf16[1,256,512]{2,1,0:T(8,128)(2,1)S(1)}, u32[]{:S(2)}, u32[]{:S(2)}) collective-permute-start(bf16[1,256,512]{2,1,0:T(8,128)(2,1)S(1)} %get-tuple-element.19), channel_id=1, source_target_pairs={{0,16},{4,20},{8,24},{12,28},{16,0},{20,4},{24,8},{28,12},{1,17},{... | collective-permute-start | bytes 786440 | tf_op jit(solution)/shard_map/ppermute | solution.py:277
  4.8 1.5 %collective-permute-start.1 = (bf16[1,256,512]{2,1,0:T(8,128)(2,1)S(1)}, bf16[1,256,512]{2,1,0:T(8,128)(2,1)S(1)}, u32[]{:S(2)}, u32[]{:S(2)}) collective-permute-start(bf16[1,256,512]{2,1,0:T(8,128)(2,1)S(1)} %get-tuple-element.20), channel_id=1, source_target_pairs={{0,8},{4,12},{8,0},{12,4},{16,24},{20,28},{24,16},{28,20},{1,9},{5... | collective-permute-start | bytes 786440 | tf_op jit(solution)/shard_map/ppermute | solution.py:277
  6.2 2.7 %constant_dynamic-slice_fusion.13 = (bf16[3,256,512]{2,1,0:T(8,128)(2,1)}, bf16[3,256,512]{2,1,0:T(8,128)(2,1)}) fusion(bf16[32,256,512]{2,1,0:T(8,128)(2,1)} %chol_ref.3, s32[]{:T(128)S(6)} %select_n.46, s32[]{:T(128)S(6)} %select_n.45), kind=kLoop, calls=%fused_computation.18 | loop fusion | bytes 3145736 | tf_op jit(solution)/shard_map/dynamic_slice | solution.py:280
  9.0 4.1 %constant_dynamic-slice_fusion.9 = (bf16[4,256,512]{2,1,0:T(8,128)(2,1)}, bf16[4,256,512]{2,1,0:T(8,128)(2,1)S(1)}, bf16[4,256,512]{2,1,0:T(8,128)(2,1)S(1)}, bf16[4,256,512]{2,1,0:T(8,128)(2,1)}) fusion(bf16[32,256,512]{2,1,0:T(8,128)(2,1)} %chol_ref.3, s32[]{:T(128)S(6)} %select_n.50, s32[]{:T(128)S(6)} %select_n.49, s32[]{:T(128)S(6)} %select_n.48, ...), kind=kLoop, calls=%fused_computation.14 | loop fusion | bytes 8388624 | tf_op jit(solution)/shard_map/dynamic_slice | solution.py:280
  13.1 2.5 %fusion.2 = bf16[256,2048]{1,0:T(8,128)(2,1)S(1)} fusion(bf16[1,1024,2048]{2,1,0:T(8,128)(2,1)S(1)} %copy-done.4, bf16[2048,1024]{1,0:T(8,128)(2,1)} %source_ref.1, s32[]{:T(128)S(6)} %select_n.51), kind=kOutput, calls=%fused_computation.2 | convolution fusion | flops 1074266112 | bytes 5767172 | tf_op jit(solution)/shard_map/dot_general | solution.py:301
  16.5 3.6 %collective-permute-start.4 = (bf16[256,512]{1,0:T(8,128)(2,1)}, bf16[256,512]{1,0:T(8,128)(2,1)S(1)}, u32[]{:S(2)}, u32[]{:S(2)}) collective-permute-start(bf16[256,512]{1,0:T(8,128)(2,1)} %get-tuple-element.46), channel_id=1, source_target_pairs={{0,3},{1,2},{2,1},{3,0},{4,7},{5,6},{6,5},{7,4},{8,11},{9,10},{10,... | collective-permute-start | bytes 786440 | tf_op jit(solution)/shard_map/ppermute | solution.py:277
  22.3 5.5 %collective-permute-done.4.refs_3_ = bf16[256,512]{1,0:T(8,128)(2,1)S(1)} collective-permute-done((bf16[256,512]{1,0:T(8,128)(2,1)}, bf16[256,512]{1,0:T(8,128)(2,1)S(1)}, u32[]{:S(2)}, u32[]{:S(2)}) %collective-permute-start.4) | collective-permute-done | bytes 262176 | tf_op jit(solution)/shard_map/ppermute | solution.py:277
  27.8 14.3 %collective-permute-done.3.refs_2_ = bf16[256,512]{1,0:T(8,128)(2,1)S(1)} collective-permute-done((bf16[256,512]{1,0:T(8,128)(2,1)}, bf16[256,512]{1,0:T(8,128)(2,1)S(1)}, u32[]{:S(2)}, u32[]{:S(2)}) %collective-permute-start.3) | collective-permute-done | bytes 262176 | tf_op jit(solution)/shard_map/ppermute | solution.py:277
  42.1 7.3 %terms.1 = f32[4,32,1,512]{3,2,1,0:T(1,128)S(1)} custom-call(s32[2]{0:T(128)S(1)} %pad_add_fusion.place, bf16[32,256,512]{2,1,0:T(8,128)(2,1)} %chol_ref.3, bf16[256,512]{1,0:T(8,128)(2,1)S(1)} %get-tuple-element.49.refs_0_, bf16[256,512]{1,0:T(8,128)(2,1)S(1)} %collective-permute-done.2.refs_1_, bf16[256,512]{1,0:T(8,128)(2,1)S(1)} %collective-permute-done.3.refs_2_, ...), custom_call_target="tpu_custom_call" | custom-call | flops 33554432 | bytes 8388608 | tf_op jit(solution)/shard_map/terms/pallas_call | solution.py:80
  49.9 2.5 %collective-permute-start.7 = (f32[32]{0:T(128)S(1)}, f32[32]{0:T(128)S(1)}, u32[]{:S(2)}, u32[]{:S(2)}) collective-permute-start(f32[32]{0:T(128)S(1)} %get-tuple-element.54), channel_id=1, source_target_pairs={{0,3},{1,2},{2,1},{3,0},{4,7},{5,6},{6,5},{7,4},{8,11},{9,10},{10,... | collective-permute-start | bytes 392 | tf_op jit(solution)/shard_map/ppermute | solution.py:277
  52.4 1.9 %collective-permute-done.6 = f32[32]{0:T(128)S(1)} collective-permute-done((f32[32]{0:T(128)S(1)}, f32[32]{0:T(128)S(1)}, u32[]{:S(2)}, u32[]{:S(2)}) %collective-permute-start.6) | collective-permute-done | bytes 160 | tf_op jit(solution)/shard_map/ppermute | solution.py:277
  55.3 2.6 %collective-permute-done.5 = f32[32]{0:T(128)S(1)} collective-permute-done((f32[32]{0:T(128)S(1)}, f32[32]{0:T(128)S(1)}, u32[]{:S(2)}, u32[]{:S(2)}) %collective-permute-start.5) | collective-permute-done | bytes 160 | tf_op jit(solution)/shard_map/ppermute | solution.py:277
  58.1 1.1 collective-permute-done.8
  59.5 2.7 %constant_dynamic-slice_fusion.3 = (bf16[3,256,512]{2,1,0:T(8,128)(2,1)}, bf16[3,256,512]{2,1,0:T(8,128)(2,1)}) fusion(bf16[32,256,512]{2,1,0:T(8,128)(2,1)} %chol_ref.3, s32[]{:T(128)S(6)} %select_n.57, s32[]{:T(128)S(6)} %select_n.56), kind=kLoop, calls=%fused_computation.7 | loop fusion | bytes 3145736 | tf_op jit(solution)/shard_map/dynamic_slice | solution.py:280
  62.3 2.2 %copy-done = bf16[2048,1024]{1,0:T(8,128)(2,1)S(1)} copy-done((bf16[2048,1024]{1,0:T(8,128)(2,1)S(1)}, bf16[2048,1024]{1,0:T(8,128)(2,1)}, u32[]{:S(2)}) %copy-start) | copy-done | bytes 4194328
  64.5 1.0 turn.3.lhs_ref
  65.5 1.1 copy-done.1
  66.7 2.0 %turn.2.lhs_ref = bf16[1024,1536]{1,0:T(8,128)(2,1)S(1)} custom-call(s32[6]{0:T(128)S(1)} %broadcast_xor_fusion.1.place, bf16[2048,1024]{1,0:T(8,128)(2,1)S(1)} %copy-done.1), custom_call_target="tpu_custom_call" | custom-call | flops 471859200 | bytes 6291456 | tf_op jit(solution)/shard_map/turn/pallas_call | solution.py:103
  68.6 1.7 %copy-done.2 = bf16[1024,1536]{1,0:T(8,128)(2,1)} copy-done((bf16[1024,1536]{1,0:T(8,128)(2,1)}, bf16[1024,1536]{1,0:T(8,128)(2,1)S(1)}, u32[]{:S(2)}) %copy-start.2) | copy-done | bytes 3145752
  70.3 1.5 %collective-permute-start.21 = (bf16[3,256,512]{2,1,0:T(8,128)(2,1)}, bf16[3,256,512]{2,1,0:T(8,128)(2,1)S(1)}, u32[]{:S(2)}, u32[]{:S(2)}) collective-permute-start(bf16[3,256,512]{2,1,0:T(8,128)(2,1)} %get-tuple-element.38), channel_id=1, source_target_pairs={{0,28},{4,24},{8,20},{12,16},{16,12},{20,8},{24,4},{28,0},{1,29},{... | collective-permute-start | bytes 2359304 | tf_op jit(solution)/shard_map/ppermute | solution.py:277
  71.8 1.4 %collective-permute-start.20 = (bf16[3,256,512]{2,1,0:T(8,128)(2,1)}, bf16[3,256,512]{2,1,0:T(8,128)(2,1)S(1)}, u32[]{:S(2)}, u32[]{:S(2)}) collective-permute-start(bf16[3,256,512]{2,1,0:T(8,128)(2,1)} %get-tuple-element.39), channel_id=1, source_target_pairs={{0,24},{4,28},{8,16},{12,20},{16,8},{20,12},{24,0},{28,4},{1,25},{... | collective-permute-start | bytes 2359304 | tf_op jit(solution)/shard_map/ppermute | solution.py:277
  75.2 1.6 %collective-permute-start.11 = (f32[1,4]{1,0:T(1,128)S(1)}, f32[1,4]{1,0:T(1,128)S(1)}, u32[]{:S(2)}, u32[]{:S(2)}) collective-permute-start(f32[1,4]{1,0:T(1,128)S(1)} %get-tuple-element.50), channel_id=1, source_target_pairs={{0,24},{4,28},{8,16},{12,20},{16,8},{20,12},{24,0},{28,4},{1,25},{... | collective-permute-start | bytes 56 | tf_op jit(solution)/shard_map/ppermute | solution.py:277
  76.8 4.1 %collective-permute-done.15.refs_6_ = bf16[4,256,512]{2,1,0:T(8,128)(2,1)} collective-permute-done((bf16[4,256,512]{2,1,0:T(8,128)(2,1)S(1)}, bf16[4,256,512]{2,1,0:T(8,128)(2,1)}, u32[]{:S(2)}, u32[]{:S(2)}) %collective-permute-start.15) | collective-permute-done | bytes 1048608 | tf_op jit(solution)/shard_map/ppermute | solution.py:277
  81.4 36.8 %collective-permute-done.14.refs_5_ = bf16[4,256,512]{2,1,0:T(8,128)(2,1)} collective-permute-done((bf16[4,256,512]{2,1,0:T(8,128)(2,1)S(1)}, bf16[4,256,512]{2,1,0:T(8,128)(2,1)}, u32[]{:S(2)}, u32[]{:S(2)}) %collective-permute-start.14) | collective-permute-done | bytes 1048608 | tf_op jit(solution)/shard_map/ppermute | solution.py:277
  118.7 10.5 %near.1.near_ref = f32[4,1024,512]{2,1,0:T(8,128)S(1)} custom-call(bf16[1024,1536]{1,0:T(8,128)(2,1)} %copy-done.2, bf16[4,256,512]{2,1,0:T(8,128)(2,1)} %get-tuple-element.43.refs_0_, bf16[1,256,512]{2,1,0:T(8,128)(2,1)} %copy-done.5, bf16[3,256,512]{2,1,0:T(8,128)(2,1)} %collective-permute-done.12.refs_2_, bf16[1,256,512]{2,1,0:T(8,128)(2,1)} %copy-done.6, ...), custom_call_target="tpu_custom_call" | custom-call | flops 6442450944 | bytes 8388608 | tf_op jit(solution)/shard_map/near/pallas_call | solution.py:147
  129.2 1.6 %collective-permute-start.9 = (f32[1,4]{1,0:T(1,128)S(1)}, f32[1,4]{1,0:T(1,128)S(1)}, u32[]{:S(2)}, u32[]{:S(2)}) collective-permute-start(f32[1,4]{1,0:T(1,128)S(1)} %get-tuple-element.52), channel_id=1, source_target_pairs={{0,8},{4,12},{8,0},{12,4},{16,24},{20,28},{24,16},{28,20},{1,9},{5... | collective-permute-start | bytes 56 | tf_op jit(solution)/shard_map/ppermute | solution.py:277
  131.4 1.4 collective-permute-done.9
  134.0 2.6 %far.1._ = bf16[4,1024,512]{2,1,0:T(8,128)(2,1)} custom-call(bf16[1024,512]{1,0:T(8,128)(2,1)S(1)} %turn.3.lhs_ref, f32[4,1024,512]{2,1,0:T(8,128)S(1)} %near.1.near_ref, bf16[3,256,512]{2,1,0:T(8,128)(2,1)S(1)} %collective-permute-done.20.refs_0_, bf16[3,256,512]{2,1,0:T(8,128)(2,1)S(1)} %collective-permute-done.21.refs_1_), custom_call_target="tpu_custom_call" | custom-call | flops 1610612736 | bytes 6291456 | tf_op jit(solution)/shard_map/far/pallas_call | solution.py:185
  137.4 1.1 last.2._
  139.0 1.0 collective-permute-done.18.block_ref
  140.0 1.1 last.3
  (58 shorter events, 11.3 us)
Async XLA Ops:
  1.7 11.4 %collective-permute-start = (bf16[1,256,512]{2,1,0:T(8,128)(2,1)S(1)}, bf16[1,256,512]{2,1,0:T(8,128)(2,1)S(1)}, u32[]{:S(2)}, u32[]{:S(2)}) collective-permute-start(bf16[1,256,512]{2,1,0:T(8,128)(2,1)S(1)} %get-tuple-element.19), channel_id=1, source_target_pairs={{0,16},{4,20},{8,24},{12,28},{16,0},{20,4},{24,8},{28,12},{1,17},{... | collective-permute-start | bytes 786440 | tf_op jit(solution)/shard_map/ppermute | solution.py:277
  4.8 8.3 %collective-permute-start.1 = (bf16[1,256,512]{2,1,0:T(8,128)(2,1)S(1)}, bf16[1,256,512]{2,1,0:T(8,128)(2,1)S(1)}, u32[]{:S(2)}, u32[]{:S(2)}) collective-permute-start(bf16[1,256,512]{2,1,0:T(8,128)(2,1)S(1)} %get-tuple-element.20), channel_id=1, source_target_pairs={{0,8},{4,12},{8,0},{12,4},{16,24},{20,28},{24,16},{28,20},{1,9},{5... | collective-permute-start | bytes 786440 | tf_op jit(solution)/shard_map/ppermute | solution.py:277
  9.0 4.1 %copy-start.4 = (bf16[1,1024,2048]{2,1,0:T(8,128)(2,1)S(1)}, bf16[1,1024,2048]{2,1,0:T(8,128)(2,1)}, u32[]{:S(2)}) copy-start(bf16[1,1024,2048]{2,1,0:T(8,128)(2,1)} %param.8) | copy-start | bytes 12582916
  13.1 3.4 %copy-start.5 = (bf16[1,256,512]{2,1,0:T(8,128)(2,1)}, bf16[1,256,512]{2,1,0:T(8,128)(2,1)S(1)}, u32[]{:S(2)}) copy-start(bf16[1,256,512]{2,1,0:T(8,128)(2,1)S(1)} %collective-permute-done.refs_1_) | copy-start | bytes 786436
  13.1 3.4 %copy-start.6 = (bf16[1,256,512]{2,1,0:T(8,128)(2,1)}, bf16[1,256,512]{2,1,0:T(8,128)(2,1)S(1)}, u32[]{:S(2)}) copy-start(bf16[1,256,512]{2,1,0:T(8,128)(2,1)S(1)} %collective-permute-done.1.refs_3_) | copy-start | bytes 786436
  16.5 11.3 %collective-permute-start.4 = (bf16[256,512]{1,0:T(8,128)(2,1)}, bf16[256,512]{1,0:T(8,128)(2,1)S(1)}, u32[]{:S(2)}, u32[]{:S(2)}) collective-permute-start(bf16[256,512]{1,0:T(8,128)(2,1)} %get-tuple-element.46), channel_id=1, source_target_pairs={{0,3},{1,2},{2,1},{3,0},{4,7},{5,6},{6,5},{7,4},{8,11},{9,10},{10,... | collective-permute-start | bytes 786440 | tf_op jit(solution)/shard_map/ppermute | solution.py:277
  20.1 22.0 %collective-permute-start.3 = (bf16[256,512]{1,0:T(8,128)(2,1)}, bf16[256,512]{1,0:T(8,128)(2,1)S(1)}, u32[]{:S(2)}, u32[]{:S(2)}) collective-permute-start(bf16[256,512]{1,0:T(8,128)(2,1)} %get-tuple-element.47), channel_id=1, source_target_pairs={{0,2},{1,3},{2,0},{3,1},{4,6},{5,7},{6,4},{7,5},{8,10},{9,11},{10,... | collective-permute-start | bytes 786440 | tf_op jit(solution)/shard_map/ppermute | solution.py:277
  20.1 22.0 %collective-permute-start.2 = (bf16[256,512]{1,0:T(8,128)(2,1)S(1)}, bf16[256,512]{1,0:T(8,128)(2,1)S(1)}, u32[]{:S(2)}, u32[]{:S(2)}) collective-permute-start(bf16[256,512]{1,0:T(8,128)(2,1)S(1)} %get-tuple-element.48), channel_id=1, source_target_pairs={{0,1},{1,0},{2,3},{3,2},{4,5},{5,4},{6,7},{7,6},{8,9},{9,8},{10,11... | collective-permute-start | bytes 786440 | tf_op jit(solution)/shard_map/ppermute | solution.py:277
  20.9 49.4 %collective-permute-start.13 = (bf16[3,256,512]{2,1,0:T(8,128)(2,1)}, bf16[3,256,512]{2,1,0:T(8,128)(2,1)}, u32[]{:S(2)}, u32[]{:S(2)}) collective-permute-start(bf16[3,256,512]{2,1,0:T(8,128)(2,1)} %get-tuple-element.44), channel_id=1, source_target_pairs={{0,8},{4,12},{8,0},{12,4},{16,24},{20,28},{24,16},{28,20},{1,9},{5... | collective-permute-start | bytes 2359304 | tf_op jit(solution)/shard_map/ppermute | solution.py:277
  21.7 50.1 %collective-permute-start.12 = (bf16[3,256,512]{2,1,0:T(8,128)(2,1)}, bf16[3,256,512]{2,1,0:T(8,128)(2,1)}, u32[]{:S(2)}, u32[]{:S(2)}) collective-permute-start(bf16[3,256,512]{2,1,0:T(8,128)(2,1)} %get-tuple-element.45), channel_id=1, source_target_pairs={{0,16},{4,20},{8,24},{12,28},{16,0},{20,4},{24,8},{28,12},{1,17},{... | collective-permute-start | bytes 2359304 | tf_op jit(solution)/shard_map/ppermute | solution.py:277
  27.8 47.4 %collective-permute-start.16 = (bf16[4,256,512]{2,1,0:T(8,128)(2,1)}, bf16[4,256,512]{2,1,0:T(8,128)(2,1)}, u32[]{:S(2)}, u32[]{:S(2)}) collective-permute-start(bf16[4,256,512]{2,1,0:T(8,128)(2,1)} %get-tuple-element.40), channel_id=1, source_target_pairs={{0,4},{4,0},{8,12},{12,8},{16,20},{20,16},{24,28},{28,24},{1,5},{5... | collective-permute-start | bytes 3145736 | tf_op jit(solution)/shard_map/ppermute | solution.py:277
  42.1 17.5 %copy-start.8 = (s32[6]{0:T(128)S(1)}, s32[6]{0:T(128)}, u32[]{:S(2)}) copy-start(s32[6]{0:T(128)} %constant.45.clone) | copy-start | bytes 76
  42.1 17.5 %copy-start.7 = (s32[2]{0:T(128)S(1)}, s32[2]{0:T(128)}, u32[]{:S(2)}) copy-start(s32[2]{0:T(128)} %constant.46.clone) | copy-start | bytes 28
  49.8 4.5 %collective-permute-start.6 = (f32[32]{0:T(128)S(1)}, f32[32]{0:T(128)S(1)}, u32[]{:S(2)}, u32[]{:S(2)}) collective-permute-start(f32[32]{0:T(128)S(1)} %get-tuple-element.53), channel_id=1, source_target_pairs={{0,2},{1,3},{2,0},{3,1},{4,6},{5,7},{6,4},{7,5},{8,10},{9,11},{10,... | collective-permute-start | bytes 392 | tf_op jit(solution)/shard_map/ppermute | solution.py:277
  49.9 5.4 %collective-permute-start.7 = (f32[32]{0:T(128)S(1)}, f32[32]{0:T(128)S(1)}, u32[]{:S(2)}, u32[]{:S(2)}) collective-permute-start(f32[32]{0:T(128)S(1)} %get-tuple-element.54), channel_id=1, source_target_pairs={{0,3},{1,2},{2,1},{3,0},{4,7},{5,6},{6,5},{7,4},{8,11},{9,10},{10,... | collective-permute-start | bytes 392 | tf_op jit(solution)/shard_map/ppermute | solution.py:277
  54.4 3.6 %collective-permute-start.5 = (f32[32]{0:T(128)S(1)}, f32[32]{0:T(128)S(1)}, u32[]{:S(2)}, u32[]{:S(2)}) collective-permute-start(f32[32]{0:T(128)S(1)} %get-tuple-element.55), channel_id=1, source_target_pairs={{0,1},{1,0},{2,3},{3,2},{4,5},{5,4},{6,7},{7,6},{8,9},{9,8},{10,11... | collective-permute-start | bytes 392 | tf_op jit(solution)/shard_map/ppermute | solution.py:277
  55.3 25.6 %collective-permute-start.15 = (bf16[4,256,512]{2,1,0:T(8,128)(2,1)S(1)}, bf16[4,256,512]{2,1,0:T(8,128)(2,1)}, u32[]{:S(2)}, u32[]{:S(2)}) collective-permute-start(bf16[4,256,512]{2,1,0:T(8,128)(2,1)S(1)} %get-tuple-element.41), channel_id=1, source_target_pairs={{0,12},{4,8},{8,4},{12,0},{16,28},{20,24},{24,20},{28,16},{1,13},{... | collective-permute-start | bytes 3145736 | tf_op jit(solution)/shard_map/ppermute | solution.py:277
  58.0 1.2 collective-permute-start.8
  59.3 58.9 %collective-permute-start.14 = (bf16[4,256,512]{2,1,0:T(8,128)(2,1)S(1)}, bf16[4,256,512]{2,1,0:T(8,128)(2,1)}, u32[]{:S(2)}, u32[]{:S(2)}) collective-permute-start(bf16[4,256,512]{2,1,0:T(8,128)(2,1)S(1)} %get-tuple-element.42), channel_id=1, source_target_pairs={{0,20},{4,16},{8,28},{12,24},{16,4},{20,0},{24,12},{28,8},{1,21},{... | collective-permute-start | bytes 3145736 | tf_op jit(solution)/shard_map/ppermute | solution.py:277
  62.3 2.2 %copy-start = (bf16[2048,1024]{1,0:T(8,128)(2,1)S(1)}, bf16[2048,1024]{1,0:T(8,128)(2,1)}, u32[]{:S(2)}) copy-start(bf16[2048,1024]{1,0:T(8,128)(2,1)} %source_ref.1) | copy-start | bytes 12582916
  64.5 2.2 %copy-start.1 = (bf16[2048,1024]{1,0:T(8,128)(2,1)S(1)}, bf16[2048,1024]{1,0:T(8,128)(2,1)}, u32[]{:S(2)}) copy-start(bf16[2048,1024]{1,0:T(8,128)(2,1)} %source_ref.1) | copy-start | bytes 12582916
  68.6 1.7 %copy-start.2 = (bf16[1024,1536]{1,0:T(8,128)(2,1)}, bf16[1024,1536]{1,0:T(8,128)(2,1)S(1)}, u32[]{:S(2)}) copy-start(bf16[1024,1536]{1,0:T(8,128)(2,1)S(1)} %turn.2.lhs_ref) | copy-start | bytes 9437188
  70.3 63.7 %collective-permute-start.21 = (bf16[3,256,512]{2,1,0:T(8,128)(2,1)}, bf16[3,256,512]{2,1,0:T(8,128)(2,1)S(1)}, u32[]{:S(2)}, u32[]{:S(2)}) collective-permute-start(bf16[3,256,512]{2,1,0:T(8,128)(2,1)} %get-tuple-element.38), channel_id=1, source_target_pairs={{0,28},{4,24},{8,20},{12,16},{16,12},{20,8},{24,4},{28,0},{1,29},{... | collective-permute-start | bytes 2359304 | tf_op jit(solution)/shard_map/ppermute | solution.py:277
  71.8 62.2 %collective-permute-start.20 = (bf16[3,256,512]{2,1,0:T(8,128)(2,1)}, bf16[3,256,512]{2,1,0:T(8,128)(2,1)S(1)}, u32[]{:S(2)}, u32[]{:S(2)}) collective-permute-start(bf16[3,256,512]{2,1,0:T(8,128)(2,1)} %get-tuple-element.39), channel_id=1, source_target_pairs={{0,24},{4,28},{8,16},{12,20},{16,8},{20,12},{24,0},{28,4},{1,25},{... | collective-permute-start | bytes 2359304 | tf_op jit(solution)/shard_map/ppermute | solution.py:277
  75.2 53.9 %collective-permute-start.11 = (f32[1,4]{1,0:T(1,128)S(1)}, f32[1,4]{1,0:T(1,128)S(1)}, u32[]{:S(2)}, u32[]{:S(2)}) collective-permute-start(f32[1,4]{1,0:T(1,128)S(1)} %get-tuple-element.50), channel_id=1, source_target_pairs={{0,24},{4,28},{8,16},{12,20},{16,8},{20,12},{24,0},{28,4},{1,25},{... | collective-permute-start | bytes 56 | tf_op jit(solution)/shard_map/ppermute | solution.py:277
  80.9 49.8 %collective-permute-start.10 = (f32[1,4]{1,0:T(1,128)S(1)}, f32[1,4]{1,0:T(1,128)S(1)}, u32[]{:S(2)}, u32[]{:S(2)}) collective-permute-start(f32[1,4]{1,0:T(1,128)S(1)} %get-tuple-element.51), channel_id=1, source_target_pairs={{0,16},{4,20},{8,24},{12,28},{16,0},{20,4},{24,8},{28,12},{1,17},{... | collective-permute-start | bytes 56 | tf_op jit(solution)/shard_map/ppermute | solution.py:277
  118.2 15.4 %collective-permute-start.17 = (bf16[1,256,512]{2,1,0:T(8,128)(2,1)S(1)}, bf16[1,256,512]{2,1,0:T(8,128)(2,1)S(1)}, u32[]{:S(2)}, u32[]{:S(2)}) collective-permute-start(bf16[1,256,512]{2,1,0:T(8,128)(2,1)S(1)} %constant_dynamic-slice_fusion.2), channel_id=1, source_target_pairs={{0,24},{4,28},{8,16},{12,20},{16,8},{20,12},{24,0},{28,4},{1,25},{... | collective-permute-start | bytes 786440 | tf_op jit(solution)/shard_map/ppermute | solution.py:277
  129.2 3.6 %collective-permute-start.9 = (f32[1,4]{1,0:T(1,128)S(1)}, f32[1,4]{1,0:T(1,128)S(1)}, u32[]{:S(2)}, u32[]{:S(2)}) collective-permute-start(f32[1,4]{1,0:T(1,128)S(1)} %get-tuple-element.52), channel_id=1, source_target_pairs={{0,8},{4,12},{8,0},{12,4},{16,24},{20,28},{24,16},{28,20},{1,9},{5... | collective-permute-start | bytes 56 | tf_op jit(solution)/shard_map/ppermute | solution.py:277
  130.7 6.7 %collective-permute-start.19 = (bf16[1,256,256]{2,1,0:T(8,128)(2,1)S(1)}, bf16[1,256,256]{2,1,0:T(8,128)(2,1)S(1)}, u32[]{:S(2)}, u32[]{:S(2)}) collective-permute-start(bf16[1,256,256]{2,1,0:T(8,128)(2,1)S(1)} %get-tuple-element.36), channel_id=1, source_target_pairs={{0,28},{4,24},{8,20},{12,16},{16,12},{20,8},{24,4},{28,0},{1,29},{... | collective-permute-start | bytes 393224 | tf_op jit(solution)/shard_map/ppermute | solution.py:277
  132.8 7.2 %collective-permute-start.18 = (bf16[1,256,256]{2,1,0:T(8,128)(2,1)S(1)}, bf16[1,256,256]{2,1,0:T(8,128)(2,1)S(1)}, u32[]{:S(2)}, u32[]{:S(2)}) collective-permute-start(bf16[1,256,256]{2,1,0:T(8,128)(2,1)S(1)} %get-tuple-element.37), channel_id=1, source_target_pairs={{0,28},{4,24},{8,20},{12,16},{16,12},{20,8},{24,4},{28,0},{1,29},{... | collective-permute-start | bytes 393224 | tf_op jit(solution)/shard_map/ppermute | solution.py:277
  136.7 1.8 %copy-start.3 = (f32[4]{0:T(128)S(1)}, f32[4]{0:T(128)}, u32[]{:S(2)}) copy-start(f32[4]{0:T(128)} %param.9) | copy-start | bytes 52

commit v2 on v0

--- a/solution.py
+++ b/solution.py
@@ -13,10 +13,6 @@
 
 def tied(value, *after):
     return lax.optimization_barrier((value, *after))[0]
-
-
-def in_hbm(value):
-    return pltpu.with_memory_space_constraint(value, pltpu.HBM)
 
 
 def params(mib):
@@ -61,7 +57,7 @@
         compiler_params=params(8),
         cost_estimate=cost(2**20, 4 * len(offsets) * size * chol[0].size),
         name="first",
-    )(in_hbm(chol))
+    )(pltpu.with_memory_space_constraint(chol, pltpu.HBM))
 
 
 def terms_kernel(place, chol_ref, *refs):
@@ -90,7 +86,7 @@
         compiler_params=params(12),
         cost_estimate=cost(2 * walkers * chol.size, 2 * chol.size),
         name="terms",
-    )(me, in_hbm(chol), *products)
+    )(me, pltpu.with_memory_space_constraint(chol, pltpu.HBM), *products)
 
 
 def turn_kernel(place, source_ref, out_ref):
@@ -154,7 +150,7 @@
         compiler_params=params(24),
         cost_estimate=cost(2 * count * occupied * depth * columns, 4 * count * occupied * columns),
         name="near",
-    )(in_hbm(lhs), *(in_hbm(piece) for pieces in blocks for piece in pieces))
+    )(lhs, *(piece for pieces in blocks for piece in pieces))
 
 
 def far_kernel(first, blocks, lhs_ref, near_ref, *refs):
@@ -266,7 +262,7 @@
             pltpu.SemaphoreType.DMA((tiles,)),
         ],
         input_output_aliases={3: 0},
-        compiler_params=params(16),
+        compiler_params=pltpu.CompilerParams(vmem_limit_bytes=16 * MIB),
         cost_estimate=cost(2 * occupied * rows * columns, 4 * occupied * columns),
         name="last",
     )(lhs, near, block, rotated)
@@ -295,14 +291,7 @@
         for k, piece in zip(first, pieces):
             near[k].append(swap(piece, "orb", k, owners))
 
-    pieces = {k: part(source, k) for k in [0] + second}
-    source = tied(source, *pieces.values())
-    near[0] = [pieces[0]]
-    for k in second:
-        near[k] = [swap(pieces[k], "orb", k, owners)]
-
-    arrived = [near[k][0] for k in first]
-    orbitals, greens = tied((orbitals, greens), *pieces.values(), *arrived)
+    orbitals, greens = tied((orbitals, greens), *(near[k][0] for k in first))
     orbital_rows = lax.dynamic_slice_in_dim(orbitals, me * rows, rows, 0)
     products = jnp.dot(orbital_rows, greens[0], preferred_element_type=jnp.float32)
     products = products.astype(jnp.bfloat16)
@@ -312,12 +301,15 @@
     source = tied(source, *pieces)
     arrived = pieces[:1] + [swap(pieces[k], "walk", k, walkers) for k in range(1, walkers)]
 
+    pieces = {k: part(source, k) for k in [0] + second}
+    source = tied(source, *pieces.values())
+    near[0] = [pieces[0]]
+    for k in second:
+        near[k] = [swap(pieces[k], "orb", k, owners)]
+
     cuts = [(a, b) for a, b in ((0, count - 2), (count - 2, count - 1)) if a < b]
-    far = []
-    for span in cuts:
-        pieces = [part(source, k, *span) for k in far_offsets]
-        source = tied(source, *pieces)
-        far.append([swap(piece, "orb", k, owners) for k, piece in zip(far_offsets, pieces)])
+    pieces = [part(source, k, *cuts[0]) for k in far_offsets]
+    far = [[swap(piece, "orb", k, owners) for k, piece in zip(far_offsets, pieces)]]
 
     order = [0] + first + second
     lhs_near = turned(orbitals, jnp.array(order, jnp.int32) ^ me, rows)
@@ -331,6 +323,9 @@
     sums = [swap(even[k : k + 1], "orb", 2 * k, owners) for k in range(1, owners // 2)]
 
     source = tied(source, even)
+    for n, span in enumerate(cuts[1:], 1):
+        pieces = [part(source, k, *span) for k in far_offsets]
+        far.append([swap(piece, "orb", k, owners) for k, piece in zip(far_offsets, pieces)])
     pieces = [part(source, k, count - 1) for k in far_offsets]
     middle = [swap(piece, "orb", k, owners) for k, piece in zip(far_offsets[:-1], pieces)]
     half = columns // last_parts(columns)

time: 148 us -> 138 us (0.932)
  starting transfers between devices: 34.8 us -> 30.8 us
  local copies, waits for them, and re-layouts: 15.9 us -> 13.4 us
  Pallas kernels: 28.6 us -> 26.2 us
    ppermute x24, starting transfers between devices: 34.8 us -> 30.8 us  [swap(): return lax.ppermute(value, axis, [(i, i ^ k) for i in range(size)])]
    pallas_call x1, Pallas kernels: 10.5 us -> 8.74 us  [near_sum(): pl.pallas_call(functools.partial(near_kernel, counts), out_shape=jax.Shap...]
    unnamed x16, local copies, waits for them, and re-layouts: 3.87 us -> 2.21 us
    dynamic_slice x5 -> x4, local copies, waits for them, and re-layouts: 9.98 us -> 9.1 us  [part(): lax.dynamic_slice_in_dim(source, (me ^ k) * count + start, stop - start, 0)]
  transfers between devices with their start and end apart: 24 -> 24, of which waited for: 11 -> 14; matrix products, arithmetic and copies ran while one was open for 11% -> 12% of each run, Pallas kernels for 18% -> 17%
where the time goes in v2:
time: 138 us
  waiting for transfers between devices  61.7 us (45%)
  starting transfers between devices  30.8 us (22%)
  Pallas kernels  26.2 us (19%)
  local copies, waits for them, and re-layouts  13.4 us (10%)
  matrix products  3.69 us (3%)
    ppermute x24, waiting for transfers between devices, swap(): return lax.ppermute(value, axis, [(i, i ^ k) for i in range(size)])  61.7 us
    ppermute x24, starting transfers between devices, swap(): return lax.ppermute(value, axis, [(i, i ^ k) for i in range(size)])  30.8 us
    dynamic_slice x4, local copies, waits for them, and re-layouts, part(): lax.dynamic_slice_in_dim(source, (me ^ k) * count + start, stop - start, 0)  9.1 us
    pallas_call x1, Pallas kernels, near_sum(): pl.pallas_call(functools.partial(near_kernel, counts), out_shape=jax.Shap...  8.74 us
    pallas_call x1, Pallas kernels, force_terms(): pl.pallas_call(terms_kernel, out_shape=jax.ShapeDtypeStruct((walkers, vec...  7.33 us
    dot_general x1, matrix products, local(): jnp.dot(orbital_rows, greens[0], preferred_element_type=jnp.float32)  3.69 us
    pallas_call x2, Pallas kernels, far_sum(): pl.pallas_call(functools.partial(far_kernel, first, len(blocks)), out_sha...  3.49 us
    pallas_call x2, Pallas kernels, turned(): pl.pallas_call(turn_kernel, out_shape=jax.ShapeDtypeStruct((occupied, blo...  2.99 us
  transfers between devices with their start and end apart: 24, of which 14 were waited for; matrix products, arithmetic and copies ran while one was open for 12% of the time, Pallas kernels for 17%

profile of v2, /device:TPU:0, one launch (start us, length us, event | category | flops | bytes accessed | tf_op | source)
XLA Modules:
  0.0 137.6 jit_solution(6353276991751261693)
XLA Ops:
  1.7 3.1 %collective-permute-start = (bf16[1,256,512]{2,1,0:T(8,128)(2,1)S(1)}, bf16[1,256,512]{2,1,0:T(8,128)(2,1)S(1)}, u32[]{:S(2)}, u32[]{:S(2)}) collective-permute-start(bf16[1,256,512]{2,1,0:T(8,128)(2,1)S(1)} %get-tuple-element.18), channel_id=1, source_target_pairs={{0,16},{4,20},{8,24},{12,28},{16,0},{20,4},{24,8},{28,12},{1,17},{... | collective-permute-start | bytes 786440 | tf_op jit(solution)/shard_map/ppermute | solution.py:279
  4.8 1.5 %collective-permute-start.1 = (bf16[1,256,512]{2,1,0:T(8,128)(2,1)S(1)}, bf16[1,256,512]{2,1,0:T(8,128)(2,1)S(1)}, u32[]{:S(2)}, u32[]{:S(2)}) collective-permute-start(bf16[1,256,512]{2,1,0:T(8,128)(2,1)S(1)} %get-tuple-element.19), channel_id=1, source_target_pairs={{0,8},{4,12},{8,0},{12,4},{16,24},{20,28},{24,16},{28,20},{1,9},{5... | collective-permute-start | bytes 786440 | tf_op jit(solution)/shard_map/ppermute | solution.py:279
  6.2 2.7 %constant_dynamic-slice_fusion.15 = (bf16[3,256,512]{2,1,0:T(8,128)(2,1)}, bf16[3,256,512]{2,1,0:T(8,128)(2,1)}) fusion(bf16[32,256,512]{2,1,0:T(8,128)(2,1)} %chol_ref.3, s32[]{:T(128)S(6)} %select_n.52, s32[]{:T(128)S(6)} %select_n.51), kind=kLoop, calls=%fused_computation.20 | loop fusion | bytes 3145736 | tf_op jit(solution)/shard_map/dynamic_slice | solution.py:282
  9.5 2.0 %collective-permute-done.refs_1_ = bf16[1,256,512]{2,1,0:T(8,128)(2,1)S(1)} collective-permute-done((bf16[1,256,512]{2,1,0:T(8,128)(2,1)S(1)}, bf16[1,256,512]{2,1,0:T(8,128)(2,1)S(1)}, u32[]{:S(2)}, u32[]{:S(2)}) %collective-permute-start) | collective-permute-done | bytes 262176 | tf_op jit(solution)/shard_map/ppermute | solution.py:279
  12.5 3.7 %fusion.2 = bf16[256,2048]{1,0:T(8,128)(2,1)S(1)} fusion(bf16[1,1024,2048]{2,1,0:T(8,128)(2,1)} %param.8, bf16[2048,1024]{1,0:T(8,128)(2,1)} %source_ref.1, s32[]{:T(128)S(6)} %select_n.53), kind=kOutput, calls=%fused_computation.2 | convolution fusion | flops 1074266112 | bytes 5767172 | tf_op jit(solution)/shard_map/dot_general | solution.py:296
  17.1 1.6 %collective-permute-start.2 = (bf16[256,512]{1,0:T(8,128)(2,1)}, bf16[256,512]{1,0:T(8,128)(2,1)S(1)}, u32[]{:S(2)}, u32[]{:S(2)}) collective-permute-start(bf16[256,512]{1,0:T(8,128)(2,1)} %get-tuple-element.49), channel_id=1, source_target_pairs={{0,1},{1,0},{2,3},{3,2},{4,5},{5,4},{6,7},{7,6},{8,9},{9,8},{10,11... | collective-permute-start | bytes 786440 | tf_op jit(solution)/shard_map/ppermute | solution.py:279
  18.7 2.6 %collective-permute-start.3 = (bf16[256,512]{1,0:T(8,128)(2,1)}, bf16[256,512]{1,0:T(8,128)(2,1)S(1)}, u32[]{:S(2)}, u32[]{:S(2)}) collective-permute-start(bf16[256,512]{1,0:T(8,128)(2,1)} %get-tuple-element.48), channel_id=1, source_target_pairs={{0,2},{1,3},{2,0},{3,1},{4,6},{5,7},{6,4},{7,5},{8,10},{9,11},{10,... | collective-permute-start | bytes 786440 | tf_op jit(solution)/shard_map/ppermute | solution.py:279
  21.6 3.9 %constant_dynamic-slice_fusion.7 = (bf16[4,256,512]{2,1,0:T(8,128)(2,1)}, bf16[4,256,512]{2,1,0:T(8,128)(2,1)}, bf16[4,256,512]{2,1,0:T(8,128)(2,1)}, bf16[4,256,512]{2,1,0:T(8,128)(2,1)S(1)}) fusion(bf16[32,256,512]{2,1,0:T(8,128)(2,1)} %chol_ref.3, s32[]{:T(128)S(6)} %select_n.61, s32[]{:T(128)S(6)} %select_n.60, s32[]{:T(128)S(6)} %select_n.59, ...), kind=kLoop, calls=%fused_computation.11 | loop fusion | bytes 8388624 | tf_op jit(solution)/shard_map/dynamic_slice | solution.py:282
  25.5 3.0 %collective-permute-done.2.refs_1_ = bf16[256,512]{1,0:T(8,128)(2,1)S(1)} collective-permute-done((bf16[256,512]{1,0:T(8,128)(2,1)}, bf16[256,512]{1,0:T(8,128)(2,1)S(1)}, u32[]{:S(2)}, u32[]{:S(2)}) %collective-permute-start.2) | collective-permute-done | bytes 262176 | tf_op jit(solution)/shard_map/ppermute | solution.py:279
  28.5 11.7 %collective-permute-done.3.refs_2_ = bf16[256,512]{1,0:T(8,128)(2,1)S(1)} collective-permute-done((bf16[256,512]{1,0:T(8,128)(2,1)}, bf16[256,512]{1,0:T(8,128)(2,1)S(1)}, u32[]{:S(2)}, u32[]{:S(2)}) %collective-permute-start.3) | collective-permute-done | bytes 262176 | tf_op jit(solution)/shard_map/ppermute | solution.py:279
  40.2 7.3 %terms.1 = f32[4,32,1,512]{3,2,1,0:T(1,128)S(1)} custom-call(s32[2]{0:T(128)S(1)} %pad_add_fusion.place, bf16[32,256,512]{2,1,0:T(8,128)(2,1)} %chol_ref.3, bf16[256,512]{1,0:T(8,128)(2,1)S(1)} %get-tuple-element.50.refs_0_, bf16[256,512]{1,0:T(8,128)(2,1)S(1)} %collective-permute-done.2.refs_1_, bf16[256,512]{1,0:T(8,128)(2,1)S(1)} %collective-permute-done.3.refs_2_, ...), custom_call_target="tpu_custom_call" | custom-call | flops 33554432 | bytes 8388608 | tf_op jit(solution)/shard_map/terms/pallas_call | solution.py:76
  48.0 3.7 %collective-permute-start.5 = (f32[32]{0:T(128)S(1)}, f32[32]{0:T(128)S(1)}, u32[]{:S(2)}, u32[]{:S(2)}) collective-permute-start(f32[32]{0:T(128)S(1)} %get-tuple-element.56), channel_id=1, source_target_pairs={{0,1},{1,0},{2,3},{3,2},{4,5},{5,4},{6,7},{7,6},{8,9},{9,8},{10,11... | collective-permute-start | bytes 392 | tf_op jit(solution)/shard_map/ppermute | solution.py:279
  53.3 2.5 %collective-permute-start.7 = (f32[32]{0:T(128)S(1)}, f32[32]{0:T(128)S(1)}, u32[]{:S(2)}, u32[]{:S(2)}) collective-permute-start(f32[32]{0:T(128)S(1)} %get-tuple-element.55), channel_id=1, source_target_pairs={{0,3},{1,2},{2,1},{3,0},{4,7},{5,6},{6,5},{7,4},{8,11},{9,10},{10,... | collective-permute-start | bytes 392 | tf_op jit(solution)/shard_map/ppermute | solution.py:279
  56.2 2.4 %collective-permute-done.7 = f32[32]{0:T(128)S(1)} collective-permute-done((f32[32]{0:T(128)S(1)}, f32[32]{0:T(128)S(1)}, u32[]{:S(2)}, u32[]{:S(2)}) %collective-permute-start.7) | collective-permute-done | bytes 160 | tf_op jit(solution)/shard_map/ppermute | solution.py:279
  60.7 2.9 %collective-permute-done.10 = f32[1,4]{1,0:T(1,128)S(1)} collective-permute-done((f32[1,4]{1,0:T(1,128)S(1)}, f32[1,4]{1,0:T(1,128)S(1)}, u32[]{:S(2)}, u32[]{:S(2)}) %collective-permute-start.10) | collective-permute-done | bytes 48 | tf_op jit(solution)/shard_map/ppermute | solution.py:279
  63.6 1.6 %collective-permute-start.11 = (f32[1,4]{1,0:T(1,128)S(1)}, f32[1,4]{1,0:T(1,128)S(1)}, u32[]{:S(2)}, u32[]{:S(2)}) collective-permute-start(f32[1,4]{1,0:T(1,128)S(1)} %get-tuple-element.51), channel_id=1, source_target_pairs={{0,24},{4,28},{8,16},{12,20},{16,8},{20,12},{24,0},{28,4},{1,25},{... | collective-permute-start | bytes 56 | tf_op jit(solution)/shard_map/ppermute | solution.py:279
  65.2 2.9 %collective-permute-done.11 = f32[1,4]{1,0:T(1,128)S(1)} collective-permute-done((f32[1,4]{1,0:T(1,128)S(1)}, f32[1,4]{1,0:T(1,128)S(1)}, u32[]{:S(2)}, u32[]{:S(2)}) %collective-permute-start.11) | collective-permute-done | bytes 48 | tf_op jit(solution)/shard_map/ppermute | solution.py:279
  68.1 1.5 %collective-permute-start.9 = (f32[1,4]{1,0:T(1,128)S(1)}, f32[1,4]{1,0:T(1,128)S(1)}, u32[]{:S(2)}, u32[]{:S(2)}) collective-permute-start(f32[1,4]{1,0:T(1,128)S(1)} %get-tuple-element.53), channel_id=1, source_target_pairs={{0,8},{4,12},{8,0},{12,4},{16,24},{20,28},{24,16},{28,20},{1,9},{5... | collective-permute-start | bytes 56 | tf_op jit(solution)/shard_map/ppermute | solution.py:279
  69.6 2.1 %collective-permute-done.9 = f32[1,4]{1,0:T(1,128)S(1)} collective-permute-done((f32[1,4]{1,0:T(1,128)S(1)}, f32[1,4]{1,0:T(1,128)S(1)}, u32[]{:S(2)}, u32[]{:S(2)}) %collective-permute-start.9) | collective-permute-done | bytes 48 | tf_op jit(solution)/shard_map/ppermute | solution.py:279
  71.7 1.5 %collective-permute-start.13 = (bf16[3,256,512]{2,1,0:T(8,128)(2,1)}, bf16[3,256,512]{2,1,0:T(8,128)(2,1)S(1)}, u32[]{:S(2)}, u32[]{:S(2)}) collective-permute-start(bf16[3,256,512]{2,1,0:T(8,128)(2,1)} %get-tuple-element.45), channel_id=1, source_target_pairs={{0,8},{4,12},{8,0},{12,4},{16,24},{20,28},{24,16},{28,20},{1,9},{5... | collective-permute-start | bytes 2359304 | tf_op jit(solution)/shard_map/ppermute | solution.py:279
  73.2 2.2 %copy-done = bf16[2048,1024]{1,0:T(8,128)(2,1)S(1)} copy-done((bf16[2048,1024]{1,0:T(8,128)(2,1)S(1)}, bf16[2048,1024]{1,0:T(8,128)(2,1)}, u32[]{:S(2)}) %copy-start) | copy-done | bytes 4194328
  76.4 2.0 %turn.2.lhs_ref = bf16[1024,1536]{1,0:T(8,128)(2,1)S(1)} custom-call(s32[6]{0:T(128)S(1)} %broadcast_xor_fusion.1.place, bf16[2048,1024]{1,0:T(8,128)(2,1)S(1)} %copy-done), custom_call_target="tpu_custom_call" | custom-call | flops 471859200 | bytes 6291456 | tf_op jit(solution)/shard_map/turn/pallas_call | solution.py:99
  78.4 1.3 constant_dynamic-slice_fusion.1
  82.5 9.7 %collective-permute-done.13.refs_4_ = bf16[3,256,512]{2,1,0:T(8,128)(2,1)S(1)} collective-permute-done((bf16[3,256,512]{2,1,0:T(8,128)(2,1)}, bf16[3,256,512]{2,1,0:T(8,128)(2,1)S(1)}, u32[]{:S(2)}, u32[]{:S(2)}) %collective-permute-start.13) | collective-permute-done | bytes 786464 | tf_op jit(solution)/shard_map/ppermute | solution.py:279
  92.3 1.6 %collective-permute-start.20 = (bf16[1,256,512]{2,1,0:T(8,128)(2,1)S(1)}, bf16[1,256,512]{2,1,0:T(8,128)(2,1)S(1)}, u32[]{:S(2)}, u32[]{:S(2)}) collective-permute-start(bf16[1,256,512]{2,1,0:T(8,128)(2,1)S(1)} %get-tuple-element.37), channel_id=1, source_target_pairs={{0,24},{4,28},{8,16},{12,20},{16,8},{20,12},{24,0},{28,4},{1,25},{... | collective-permute-start | bytes 786440 | tf_op jit(solution)/shard_map/ppermute | solution.py:279
  93.9 2.4 %collective-permute-start.21 = (bf16[1,256,512]{2,1,0:T(8,128)(2,1)S(1)}, bf16[1,256,512]{2,1,0:T(8,128)(2,1)S(1)}, u32[]{:S(2)}, u32[]{:S(2)}) collective-permute-start(bf16[1,256,512]{2,1,0:T(8,128)(2,1)S(1)} %get-tuple-element.36), channel_id=1, source_target_pairs={{0,28},{4,24},{8,20},{12,16},{16,12},{20,8},{24,4},{28,0},{1,29},{... | collective-permute-start | bytes 786440 | tf_op jit(solution)/shard_map/ppermute | solution.py:279
  96.3 1.3 collective-permute-start.17
  97.6 8.7 %near.1.near_ref = f32[4,1024,512]{2,1,0:T(8,128)S(1)} custom-call(bf16[1024,1536]{1,0:T(8,128)(2,1)S(1)} %turn.2.lhs_ref, bf16[4,256,512]{2,1,0:T(8,128)(2,1)S(1)} %get-tuple-element.44.refs_0_, bf16[1,256,512]{2,1,0:T(8,128)(2,1)S(1)} %copy-done.2, bf16[3,256,512]{2,1,0:T(8,128)(2,1)} %collective-permute-done.12.refs_2_, ...), custom_call_target="tpu_custom_call" | custom-call | flops 6442450944 | bytes 8388608 | tf_op jit(solution)/shard_map/near/pallas_call | solution.py:143
  106.3 21.1 %collective-permute-done.17.refs_0_ = bf16[1,256,512]{2,1,0:T(8,128)(2,1)S(1)} collective-permute-done((bf16[1,256,512]{2,1,0:T(8,128)(2,1)S(1)}, bf16[1,256,512]{2,1,0:T(8,128)(2,1)S(1)}, u32[]{:S(2)}, u32[]{:S(2)}) %collective-permute-start.17) | collective-permute-done | bytes 262176 | tf_op jit(solution)/shard_map/ppermute | solution.py:279
  127.9 2.7 %collective-permute-start.18 = (bf16[1,256,256]{2,1,0:T(8,128)(2,1)S(1)}, bf16[1,256,256]{2,1,0:T(8,128)(2,1)S(1)}, u32[]{:S(2)}, u32[]{:S(2)}) collective-permute-start(bf16[1,256,256]{2,1,0:T(8,128)(2,1)S(1)} %get-tuple-element.40), channel_id=1, source_target_pairs={{0,28},{4,24},{8,20},{12,16},{16,12},{20,8},{24,4},{28,0},{1,29},{... | collective-permute-start | bytes 393224 | tf_op jit(solution)/shard_map/ppermute | solution.py:279
  130.6 2.0 %far.2.refs_2_ = bf16[4,1024,512]{2,1,0:T(8,128)(2,1)} custom-call(bf16[1024,512]{1,0:T(8,128)(2,1)S(1)} %turn.3.lhs_ref, f32[4,1024,512]{2,1,0:T(8,128)S(1)} %near.1.near_ref, bf16[2,256,512]{2,1,0:T(8,128)(2,1)S(1)} %collective-permute-done.22.refs_0_, bf16[2,256,512]{2,1,0:T(8,128)(2,1)S(1)} %collective-permute-done.23.refs_1_), custom_call_target="tpu_custom_call" | custom-call | flops 1073741824 | bytes 4194304 | tf_op jit(solution)/shard_map/far/pallas_call | solution.py:186
  132.6 1.5 %far.3._ = bf16[4,1024,512]{2,1,0:T(8,128)(2,1)} custom-call(bf16[1024,512]{1,0:T(8,128)(2,1)S(1)} %turn.3.lhs_ref, f32[4,1024,512]{2,1,0:T(8,128)S(1)} %near.1.near_ref, bf16[1,256,512]{2,1,0:T(8,128)(2,1)S(1)} %collective-permute-done.20.refs_0_, bf16[1,256,512]{2,1,0:T(8,128)(2,1)S(1)} %collective-permute-done.21.refs_1_, ...), custom_call_target="tpu_custom_call", output_to_operand_aliasing={{}: (4, {})} | custom-call | flops 536870912 | bytes 2097152 | tf_op jit(solution)/shard_map/far/pallas_call | solution.py:186
  (61 shorter events, 16.1 us)
Async XLA Ops:
  1.7 9.8 %collective-permute-start = (bf16[1,256,512]{2,1,0:T(8,128)(2,1)S(1)}, bf16[1,256,512]{2,1,0:T(8,128)(2,1)S(1)}, u32[]{:S(2)}, u32[]{:S(2)}) collective-permute-start(bf16[1,256,512]{2,1,0:T(8,128)(2,1)S(1)} %get-tuple-element.18), channel_id=1, source_target_pairs={{0,16},{4,20},{8,24},{12,28},{16,0},{20,4},{24,8},{28,12},{1,17},{... | collective-permute-start | bytes 786440 | tf_op jit(solution)/shard_map/ppermute | solution.py:279
  4.8 7.8 %collective-permute-start.1 = (bf16[1,256,512]{2,1,0:T(8,128)(2,1)S(1)}, bf16[1,256,512]{2,1,0:T(8,128)(2,1)S(1)}, u32[]{:S(2)}, u32[]{:S(2)}) collective-permute-start(bf16[1,256,512]{2,1,0:T(8,128)(2,1)S(1)} %get-tuple-element.19), channel_id=1, source_target_pairs={{0,8},{4,12},{8,0},{12,4},{16,24},{20,28},{24,16},{28,20},{1,9},{5... | collective-permute-start | bytes 786440 | tf_op jit(solution)/shard_map/ppermute | solution.py:279
  9.0 72.9 %collective-permute-start.12 = (bf16[3,256,512]{2,1,0:T(8,128)(2,1)}, bf16[3,256,512]{2,1,0:T(8,128)(2,1)}, u32[]{:S(2)}, u32[]{:S(2)}) collective-permute-start(bf16[3,256,512]{2,1,0:T(8,128)(2,1)} %get-tuple-element.46), channel_id=1, source_target_pairs={{0,16},{4,20},{8,24},{12,28},{16,0},{20,4},{24,8},{28,12},{1,17},{... | collective-permute-start | bytes 2359304 | tf_op jit(solution)/shard_map/ppermute | solution.py:279
  11.4 5.7 %copy-start.1 = (bf16[1,256,512]{2,1,0:T(8,128)(2,1)}, bf16[1,256,512]{2,1,0:T(8,128)(2,1)S(1)}, u32[]{:S(2)}) copy-start(bf16[1,256,512]{2,1,0:T(8,128)(2,1)S(1)} %collective-permute-done.refs_1_) | copy-start | bytes 786436
  12.5 4.6 %copy-start.3 = (bf16[1,256,512]{2,1,0:T(8,128)(2,1)}, bf16[1,256,512]{2,1,0:T(8,128)(2,1)S(1)}, u32[]{:S(2)}) copy-start(bf16[1,256,512]{2,1,0:T(8,128)(2,1)S(1)} %collective-permute-done.1.refs_3_) | copy-start | bytes 786436
  17.1 11.4 %collective-permute-start.2 = (bf16[256,512]{1,0:T(8,128)(2,1)}, bf16[256,512]{1,0:T(8,128)(2,1)S(1)}, u32[]{:S(2)}, u32[]{:S(2)}) collective-permute-start(bf16[256,512]{1,0:T(8,128)(2,1)} %get-tuple-element.49), channel_id=1, source_target_pairs={{0,1},{1,0},{2,3},{3,2},{4,5},{5,4},{6,7},{7,6},{8,9},{9,8},{10,11... | collective-permute-start | bytes 786440 | tf_op jit(solution)/shard_map/ppermute | solution.py:279
  18.7 21.5 %collective-permute-start.3 = (bf16[256,512]{1,0:T(8,128)(2,1)}, bf16[256,512]{1,0:T(8,128)(2,1)S(1)}, u32[]{:S(2)}, u32[]{:S(2)}) collective-permute-start(bf16[256,512]{1,0:T(8,128)(2,1)} %get-tuple-element.48), channel_id=1, source_target_pairs={{0,2},{1,3},{2,0},{3,1},{4,6},{5,7},{6,4},{7,5},{8,10},{9,11},{10,... | collective-permute-start | bytes 786440 | tf_op jit(solution)/shard_map/ppermute | solution.py:279
  21.3 18.9 %collective-permute-start.4 = (bf16[256,512]{1,0:T(8,128)(2,1)S(1)}, bf16[256,512]{1,0:T(8,128)(2,1)S(1)}, u32[]{:S(2)}, u32[]{:S(2)}) collective-permute-start(bf16[256,512]{1,0:T(8,128)(2,1)S(1)} %get-tuple-element.47), channel_id=1, source_target_pairs={{0,3},{1,2},{2,1},{3,0},{4,7},{5,6},{6,5},{7,4},{8,11},{9,10},{10,... | collective-permute-start | bytes 786440 | tf_op jit(solution)/shard_map/ppermute | solution.py:279
  25.5 66.8 %collective-permute-start.14 = (bf16[4,256,512]{2,1,0:T(8,128)(2,1)}, bf16[4,256,512]{2,1,0:T(8,128)(2,1)S(1)}, u32[]{:S(2)}, u32[]{:S(2)}) collective-permute-start(bf16[4,256,512]{2,1,0:T(8,128)(2,1)} %get-tuple-element.43), channel_id=1, source_target_pairs={{0,20},{4,16},{8,28},{12,24},{16,4},{20,0},{24,12},{28,8},{1,21},{... | collective-permute-start | bytes 3145736 | tf_op jit(solution)/shard_map/ppermute | solution.py:279
  28.5 44.7 %copy-start.7 = (s32[6]{0:T(128)S(1)}, s32[6]{0:T(128)}, u32[]{:S(2)}) copy-start(s32[6]{0:T(128)} %constant.48.clone) | copy-start | bytes 76
  28.5 44.7 %copy-start.6 = (s32[2]{0:T(128)S(1)}, s32[2]{0:T(128)}, u32[]{:S(2)}) copy-start(s32[2]{0:T(128)} %constant.49.clone) | copy-start | bytes 28
  28.5 65.4 %collective-permute-start.15 = (bf16[4,256,512]{2,1,0:T(8,128)(2,1)}, bf16[4,256,512]{2,1,0:T(8,128)(2,1)}, u32[]{:S(2)}, u32[]{:S(2)}) collective-permute-start(bf16[4,256,512]{2,1,0:T(8,128)(2,1)} %get-tuple-element.42), channel_id=1, source_target_pairs={{0,12},{4,8},{8,4},{12,0},{16,28},{20,24},{24,20},{28,16},{1,13},{... | collective-permute-start | bytes 3145736 | tf_op jit(solution)/shard_map/ppermute | solution.py:279
  48.0 5.3 %collective-permute-start.5 = (f32[32]{0:T(128)S(1)}, f32[32]{0:T(128)S(1)}, u32[]{:S(2)}, u32[]{:S(2)}) collective-permute-start(f32[32]{0:T(128)S(1)} %get-tuple-element.56), channel_id=1, source_target_pairs={{0,1},{1,0},{2,3},{3,2},{4,5},{5,4},{6,7},{7,6},{8,9},{9,8},{10,11... | collective-permute-start | bytes 392 | tf_op jit(solution)/shard_map/ppermute | solution.py:279
  51.7 4.5 %collective-permute-start.6 = (f32[32]{0:T(128)S(1)}, f32[32]{0:T(128)S(1)}, u32[]{:S(2)}, u32[]{:S(2)}) collective-permute-start(f32[32]{0:T(128)S(1)} %get-tuple-element.54), channel_id=1, source_target_pairs={{0,2},{1,3},{2,0},{3,1},{4,6},{5,7},{6,4},{7,5},{8,10},{9,11},{10,... | collective-permute-start | bytes 392 | tf_op jit(solution)/shard_map/ppermute | solution.py:279
  53.3 5.4 %collective-permute-start.7 = (f32[32]{0:T(128)S(1)}, f32[32]{0:T(128)S(1)}, u32[]{:S(2)}, u32[]{:S(2)}) collective-permute-start(f32[32]{0:T(128)S(1)} %get-tuple-element.55), channel_id=1, source_target_pairs={{0,3},{1,2},{2,1},{3,0},{4,7},{5,6},{6,5},{7,4},{8,11},{9,10},{10,... | collective-permute-start | bytes 392 | tf_op jit(solution)/shard_map/ppermute | solution.py:279
  56.2 40.0 %collective-permute-start.16 = (bf16[4,256,512]{2,1,0:T(8,128)(2,1)}, bf16[4,256,512]{2,1,0:T(8,128)(2,1)S(1)}, u32[]{:S(2)}, u32[]{:S(2)}) collective-permute-start(bf16[4,256,512]{2,1,0:T(8,128)(2,1)} %get-tuple-element.41), channel_id=1, source_target_pairs={{0,4},{4,0},{8,12},{12,8},{16,20},{20,16},{24,28},{28,24},{1,5},{5... | collective-permute-start | bytes 3145736 | tf_op jit(solution)/shard_map/ppermute | solution.py:279
  58.8 1.2 collective-permute-start.8
  60.0 3.6 %collective-permute-start.10 = (f32[1,4]{1,0:T(1,128)S(1)}, f32[1,4]{1,0:T(1,128)S(1)}, u32[]{:S(2)}, u32[]{:S(2)}) collective-permute-start(f32[1,4]{1,0:T(1,128)S(1)} %get-tuple-element.52), channel_id=1, source_target_pairs={{0,16},{4,20},{8,24},{12,28},{16,0},{20,4},{24,8},{28,12},{1,17},{... | collective-permute-start | bytes 56 | tf_op jit(solution)/shard_map/ppermute | solution.py:279
  63.6 4.5 %collective-permute-start.11 = (f32[1,4]{1,0:T(1,128)S(1)}, f32[1,4]{1,0:T(1,128)S(1)}, u32[]{:S(2)}, u32[]{:S(2)}) collective-permute-start(f32[1,4]{1,0:T(1,128)S(1)} %get-tuple-element.51), channel_id=1, source_target_pairs={{0,24},{4,28},{8,16},{12,20},{16,8},{20,12},{24,0},{28,4},{1,25},{... | collective-permute-start | bytes 56 | tf_op jit(solution)/shard_map/ppermute | solution.py:279
  68.1 3.6 %collective-permute-start.9 = (f32[1,4]{1,0:T(1,128)S(1)}, f32[1,4]{1,0:T(1,128)S(1)}, u32[]{:S(2)}, u32[]{:S(2)}) collective-permute-start(f32[1,4]{1,0:T(1,128)S(1)} %get-tuple-element.53), channel_id=1, source_target_pairs={{0,8},{4,12},{8,0},{12,4},{16,24},{20,28},{24,16},{28,20},{1,9},{5... | collective-permute-start | bytes 56 | tf_op jit(solution)/shard_map/ppermute | solution.py:279
  71.7 20.6 %collective-permute-start.13 = (bf16[3,256,512]{2,1,0:T(8,128)(2,1)}, bf16[3,256,512]{2,1,0:T(8,128)(2,1)S(1)}, u32[]{:S(2)}, u32[]{:S(2)}) collective-permute-start(bf16[3,256,512]{2,1,0:T(8,128)(2,1)} %get-tuple-element.45), channel_id=1, source_target_pairs={{0,8},{4,12},{8,0},{12,4},{16,24},{20,28},{24,16},{28,20},{1,9},{5... | collective-permute-start | bytes 2359304 | tf_op jit(solution)/shard_map/ppermute | solution.py:279
  73.2 2.2 %copy-start = (bf16[2048,1024]{1,0:T(8,128)(2,1)S(1)}, bf16[2048,1024]{1,0:T(8,128)(2,1)}, u32[]{:S(2)}) copy-start(bf16[2048,1024]{1,0:T(8,128)(2,1)} %source_ref.1) | copy-start | bytes 12582916
  76.4 21.2 %copy-start.2 = (bf16[1,256,512]{2,1,0:T(8,128)(2,1)S(1)}, bf16[1,256,512]{2,1,0:T(8,128)(2,1)}, u32[]{:S(2)}) copy-start(bf16[1,256,512]{2,1,0:T(8,128)(2,1)} %copy-done.1) | copy-start | bytes 786436
  76.4 21.2 %copy-start.4 = (bf16[1,256,512]{2,1,0:T(8,128)(2,1)S(1)}, bf16[1,256,512]{2,1,0:T(8,128)(2,1)}, u32[]{:S(2)}) copy-start(bf16[1,256,512]{2,1,0:T(8,128)(2,1)} %copy-done.3) | copy-start | bytes 786436
  81.9 46.0 %collective-permute-start.22 = (bf16[2,256,512]{2,1,0:T(8,128)(2,1)S(1)}, bf16[2,256,512]{2,1,0:T(8,128)(2,1)S(1)}, u32[]{:S(2)}, u32[]{:S(2)}) collective-permute-start(bf16[2,256,512]{2,1,0:T(8,128)(2,1)S(1)} %get-tuple-element.35), channel_id=1, source_target_pairs={{0,24},{4,28},{8,16},{12,20},{16,8},{20,12},{24,0},{28,4},{1,25},{... | collective-permute-start | bytes 1572872 | tf_op jit(solution)/shard_map/ppermute | solution.py:279
  92.3 38.3 %collective-permute-start.23 = (bf16[2,256,512]{2,1,0:T(8,128)(2,1)S(1)}, bf16[2,256,512]{2,1,0:T(8,128)(2,1)S(1)}, u32[]{:S(2)}, u32[]{:S(2)}) collective-permute-start(bf16[2,256,512]{2,1,0:T(8,128)(2,1)S(1)} %get-tuple-element.34), channel_id=1, source_target_pairs={{0,28},{4,24},{8,20},{12,16},{16,12},{20,8},{24,4},{28,0},{1,29},{... | collective-permute-start | bytes 1572872 | tf_op jit(solution)/shard_map/ppermute | solution.py:279
  92.3 40.3 %collective-permute-start.20 = (bf16[1,256,512]{2,1,0:T(8,128)(2,1)S(1)}, bf16[1,256,512]{2,1,0:T(8,128)(2,1)S(1)}, u32[]{:S(2)}, u32[]{:S(2)}) collective-permute-start(bf16[1,256,512]{2,1,0:T(8,128)(2,1)S(1)} %get-tuple-element.37), channel_id=1, source_target_pairs={{0,24},{4,28},{8,16},{12,20},{16,8},{20,12},{24,0},{28,4},{1,25},{... | collective-permute-start | bytes 786440 | tf_op jit(solution)/shard_map/ppermute | solution.py:279
  93.9 38.7 %collective-permute-start.21 = (bf16[1,256,512]{2,1,0:T(8,128)(2,1)S(1)}, bf16[1,256,512]{2,1,0:T(8,128)(2,1)S(1)}, u32[]{:S(2)}, u32[]{:S(2)}) collective-permute-start(bf16[1,256,512]{2,1,0:T(8,128)(2,1)S(1)} %get-tuple-element.36), channel_id=1, source_target_pairs={{0,28},{4,24},{8,20},{12,16},{16,12},{20,8},{24,4},{28,0},{1,29},{... | collective-permute-start | bytes 786440 | tf_op jit(solution)/shard_map/ppermute | solution.py:279
  96.3 31.1 %collective-permute-start.17 = (bf16[1,256,512]{2,1,0:T(8,128)(2,1)S(1)}, bf16[1,256,512]{2,1,0:T(8,128)(2,1)S(1)}, u32[]{:S(2)}, u32[]{:S(2)}) collective-permute-start(bf16[1,256,512]{2,1,0:T(8,128)(2,1)S(1)} %get-tuple-element.38), channel_id=1, source_target_pairs={{0,24},{4,28},{8,16},{12,20},{16,8},{20,12},{24,0},{28,4},{1,25},{... | collective-permute-start | bytes 786440 | tf_op jit(solution)/shard_map/ppermute | solution.py:279
  127.4 6.7 %collective-permute-start.19 = (bf16[1,256,256]{2,1,0:T(8,128)(2,1)S(1)}, bf16[1,256,256]{2,1,0:T(8,128)(2,1)S(1)}, u32[]{:S(2)}, u32[]{:S(2)}) collective-permute-start(bf16[1,256,256]{2,1,0:T(8,128)(2,1)S(1)} %get-tuple-element.39), channel_id=1, source_target_pairs={{0,28},{4,24},{8,20},{12,16},{16,12},{20,8},{24,4},{28,0},{1,29},{... | collective-permute-start | bytes 393224 | tf_op jit(solution)/shard_map/ppermute | solution.py:279
  127.9 8.6 %collective-permute-start.18 = (bf16[1,256,256]{2,1,0:T(8,128)(2,1)S(1)}, bf16[1,256,256]{2,1,0:T(8,128)(2,1)S(1)}, u32[]{:S(2)}, u32[]{:S(2)}) collective-permute-start(bf16[1,256,256]{2,1,0:T(8,128)(2,1)S(1)} %get-tuple-element.40), channel_id=1, source_target_pairs={{0,28},{4,24},{8,20},{12,16},{16,12},{20,8},{24,4},{28,0},{1,29},{... | collective-permute-start | bytes 393224 | tf_op jit(solution)/shard_map/ppermute | solution.py:279
  134.1 1.1 copy-start.5

commit v3 on v2

--- a/solution.py
+++ b/solution.py
@@ -26,8 +26,8 @@
     return first, second, [k for k in range(1, owners) if chips(k) > 1]
 
 
-def last_parts(columns):
-    return 2 if columns % 256 == 0 else 1
+def last_parts():
+    return 1
 
 
 def cost(flops, moved):
@@ -262,7 +262,7 @@
             pltpu.SemaphoreType.DMA((tiles,)),
         ],
         input_output_aliases={3: 0},
-        compiler_params=pltpu.CompilerParams(vmem_limit_bytes=16 * MIB),
+        compiler_params=params(16),
         cost_estimate=cost(2 * occupied * rows * columns, 4 * occupied * columns),
         name="last",
     )(lhs, near, block, rotated)
@@ -328,7 +328,7 @@
         far.append([swap(piece, "orb", k, owners) for k, piece in zip(far_offsets, pieces)])
     pieces = [part(source, k, count - 1) for k in far_offsets]
     middle = [swap(piece, "orb", k, owners) for k, piece in zip(far_offsets[:-1], pieces)]
-    half = columns // last_parts(columns)
+    half = columns // last_parts()
     last = [
         swap(pieces[-1][..., at : at + half], "orb", far_offsets[-1], owners)
         for at in range(0, columns, half)

time: 138 us -> 139 us (level)
  waiting for transfers between devices: 61.7 us -> 66.6 us
  starting transfers between devices: 30.8 us -> 28.1 us
    ppermute x24 -> x23, waiting for transfers between devices: 61.7 us -> 66.6 us  [swap(): return lax.ppermute(value, axis, [(i, i ^ k) for i in range(size)])]
    ppermute x24 -> x23, starting transfers between devices: 30.8 us -> 28.1 us  [swap(): return lax.ppermute(value, axis, [(i, i ^ k) for i in range(size)])]
  transfers between devices with their start and end apart: 24 -> 23, of which waited for: 14 -> 14; matrix products, arithmetic and copies ran while one was open for 12% -> 11% of each run, Pallas kernels for 17% -> 17%
where the time goes in v3:
time: 139 us; the launch traced here: 138 us
  waiting for transfers between devices  66.6 us (48%)
  starting transfers between devices  28.1 us (20%)
  Pallas kernels  25.4 us (18%)
  local copies, waits for them, and re-layouts  12.5 us (9%)
  matrix products  3.69 us (3%)
    ppermute x23, waiting for transfers between devices, swap(): return lax.ppermute(value, axis, [(i, i ^ k) for i in range(size)])  66.6 us
    ppermute x23, starting transfers between devices, swap(): return lax.ppermute(value, axis, [(i, i ^ k) for i in range(size)])  28.1 us
    dynamic_slice x4, local copies, waits for them, and re-layouts, part(): lax.dynamic_slice_in_dim(source, (me ^ k) * count + start, stop - start, 0)  9.21 us
    pallas_call x1, Pallas kernels, near_sum(): pl.pallas_call(functools.partial(near_kernel, counts), out_shape=jax.Shap...  8.83 us
    pallas_call x1, Pallas kernels, force_terms(): pl.pallas_call(terms_kernel, out_shape=jax.ShapeDtypeStruct((walkers, vec...  7.33 us
    dot_general x1, matrix products, local(): jnp.dot(orbital_rows, greens[0], preferred_element_type=jnp.float32)  3.69 us
    pallas_call x2, Pallas kernels, far_sum(): pl.pallas_call(functools.partial(far_kernel, first, len(blocks)), out_sha...  3.49 us
    pallas_call x2, Pallas kernels, turned(): pl.pallas_call(turn_kernel, out_shape=jax.ShapeDtypeStruct((occupied, blo...  2.99 us
  transfers between devices with their start and end apart: 23, of which 14 were waited for; matrix products, arithmetic and copies ran while one was open for 11% of the time, Pallas kernels for 17%

profile of v3, /device:TPU:0, one launch (start us, length us, event | category | flops | bytes accessed | tf_op | source)
XLA Modules:
  0.0 138.1 jit_solution(7890987043814364461)
XLA Ops:
  1.7 3.1 %collective-permute-start = (bf16[1,256,512]{2,1,0:T(8,128)(2,1)S(1)}, bf16[1,256,512]{2,1,0:T(8,128)(2,1)S(1)}, u32[]{:S(2)}, u32[]{:S(2)}) collective-permute-start(bf16[1,256,512]{2,1,0:T(8,128)(2,1)S(1)} %get-tuple-element.18), channel_id=1, source_target_pairs={{0,16},{4,20},{8,24},{12,28},{16,0},{20,4},{24,8},{28,12},{1,17},{... | collective-permute-start | bytes 786440 | tf_op jit(solution)/shard_map/ppermute | solution.py:279
  4.8 1.5 %collective-permute-start.1 = (bf16[1,256,512]{2,1,0:T(8,128)(2,1)S(1)}, bf16[1,256,512]{2,1,0:T(8,128)(2,1)S(1)}, u32[]{:S(2)}, u32[]{:S(2)}) collective-permute-start(bf16[1,256,512]{2,1,0:T(8,128)(2,1)S(1)} %get-tuple-element.19), channel_id=1, source_target_pairs={{0,8},{4,12},{8,0},{12,4},{16,24},{20,28},{24,16},{28,20},{1,9},{5... | collective-permute-start | bytes 786440 | tf_op jit(solution)/shard_map/ppermute | solution.py:279
  6.2 2.8 %constant_dynamic-slice_fusion.14 = (bf16[3,256,512]{2,1,0:T(8,128)(2,1)}, bf16[3,256,512]{2,1,0:T(8,128)(2,1)}) fusion(bf16[32,256,512]{2,1,0:T(8,128)(2,1)} %chol_ref.3, s32[]{:T(128)S(6)} %select_n.52, s32[]{:T(128)S(6)} %select_n.51), kind=kLoop, calls=%fused_computation.19 | loop fusion | bytes 3145736 | tf_op jit(solution)/shard_map/dynamic_slice | solution.py:282
  9.5 1.9 %collective-permute-done.refs_1_ = bf16[1,256,512]{2,1,0:T(8,128)(2,1)S(1)} collective-permute-done((bf16[1,256,512]{2,1,0:T(8,128)(2,1)S(1)}, bf16[1,256,512]{2,1,0:T(8,128)(2,1)S(1)}, u32[]{:S(2)}, u32[]{:S(2)}) %collective-permute-start) | collective-permute-done | bytes 262176 | tf_op jit(solution)/shard_map/ppermute | solution.py:279
  12.5 3.7 %fusion.2 = bf16[256,2048]{1,0:T(8,128)(2,1)S(1)} fusion(bf16[1,1024,2048]{2,1,0:T(8,128)(2,1)} %param.8, bf16[2048,1024]{1,0:T(8,128)(2,1)} %source_ref.1, s32[]{:T(128)S(6)} %select_n.53), kind=kOutput, calls=%fused_computation.2 | convolution fusion | flops 1074266112 | bytes 5767172 | tf_op jit(solution)/shard_map/dot_general | solution.py:296
  17.1 1.6 %collective-permute-start.2 = (bf16[256,512]{1,0:T(8,128)(2,1)}, bf16[256,512]{1,0:T(8,128)(2,1)S(1)}, u32[]{:S(2)}, u32[]{:S(2)}) collective-permute-start(bf16[256,512]{1,0:T(8,128)(2,1)} %get-tuple-element.48), channel_id=1, source_target_pairs={{0,1},{1,0},{2,3},{3,2},{4,5},{5,4},{6,7},{7,6},{8,9},{9,8},{10,11... | collective-permute-start | bytes 786440 | tf_op jit(solution)/shard_map/ppermute | solution.py:279
  18.7 2.6 %collective-permute-start.3 = (bf16[256,512]{1,0:T(8,128)(2,1)}, bf16[256,512]{1,0:T(8,128)(2,1)S(1)}, u32[]{:S(2)}, u32[]{:S(2)}) collective-permute-start(bf16[256,512]{1,0:T(8,128)(2,1)} %get-tuple-element.47), channel_id=1, source_target_pairs={{0,2},{1,3},{2,0},{3,1},{4,6},{5,7},{6,4},{7,5},{8,10},{9,11},{10,... | collective-permute-start | bytes 786440 | tf_op jit(solution)/shard_map/ppermute | solution.py:279
  21.6 3.9 %constant_dynamic-slice_fusion.6 = (bf16[4,256,512]{2,1,0:T(8,128)(2,1)}, bf16[4,256,512]{2,1,0:T(8,128)(2,1)}, bf16[4,256,512]{2,1,0:T(8,128)(2,1)}, bf16[4,256,512]{2,1,0:T(8,128)(2,1)S(1)}) fusion(bf16[32,256,512]{2,1,0:T(8,128)(2,1)} %chol_ref.3, s32[]{:T(128)S(6)} %select_n.61, s32[]{:T(128)S(6)} %select_n.60, s32[]{:T(128)S(6)} %select_n.59, ...), kind=kLoop, calls=%fused_computation.10 | loop fusion | bytes 8388624 | tf_op jit(solution)/shard_map/dynamic_slice | solution.py:282
  25.5 3.0 %collective-permute-done.2.refs_1_ = bf16[256,512]{1,0:T(8,128)(2,1)S(1)} collective-permute-done((bf16[256,512]{1,0:T(8,128)(2,1)}, bf16[256,512]{1,0:T(8,128)(2,1)S(1)}, u32[]{:S(2)}, u32[]{:S(2)}) %collective-permute-start.2) | collective-permute-done | bytes 262176 | tf_op jit(solution)/shard_map/ppermute | solution.py:279
  28.5 11.7 %collective-permute-done.3.refs_2_ = bf16[256,512]{1,0:T(8,128)(2,1)S(1)} collective-permute-done((bf16[256,512]{1,0:T(8,128)(2,1)}, bf16[256,512]{1,0:T(8,128)(2,1)S(1)}, u32[]{:S(2)}, u32[]{:S(2)}) %collective-permute-start.3) | collective-permute-done | bytes 262176 | tf_op jit(solution)/shard_map/ppermute | solution.py:279
  40.3 7.3 %terms.1 = f32[4,32,1,512]{3,2,1,0:T(1,128)S(1)} custom-call(s32[2]{0:T(128)S(1)} %pad_add_fusion.place, bf16[32,256,512]{2,1,0:T(8,128)(2,1)} %chol_ref.3, bf16[256,512]{1,0:T(8,128)(2,1)S(1)} %get-tuple-element.49.refs_0_, bf16[256,512]{1,0:T(8,128)(2,1)S(1)} %collective-permute-done.2.refs_1_, bf16[256,512]{1,0:T(8,128)(2,1)S(1)} %collective-permute-done.3.refs_2_, ...), custom_call_target="tpu_custom_call" | custom-call | flops 33554432 | bytes 8388608 | tf_op jit(solution)/shard_map/terms/pallas_call | solution.py:76
  48.0 3.7 %collective-permute-start.5 = (f32[32]{0:T(128)S(1)}, f32[32]{0:T(128)S(1)}, u32[]{:S(2)}, u32[]{:S(2)}) collective-permute-start(f32[32]{0:T(128)S(1)} %get-tuple-element.55), channel_id=1, source_target_pairs={{0,1},{1,0},{2,3},{3,2},{4,5},{5,4},{6,7},{7,6},{8,9},{9,8},{10,11... | collective-permute-start | bytes 392 | tf_op jit(solution)/shard_map/ppermute | solution.py:279
  53.3 2.5 %collective-permute-start.7 = (f32[32]{0:T(128)S(1)}, f32[32]{0:T(128)S(1)}, u32[]{:S(2)}, u32[]{:S(2)}) collective-permute-start(f32[32]{0:T(128)S(1)} %get-tuple-element.54), channel_id=1, source_target_pairs={{0,3},{1,2},{2,1},{3,0},{4,7},{5,6},{6,5},{7,4},{8,11},{9,10},{10,... | collective-permute-start | bytes 392 | tf_op jit(solution)/shard_map/ppermute | solution.py:279
  56.2 2.4 %collective-permute-done.7 = f32[32]{0:T(128)S(1)} collective-permute-done((f32[32]{0:T(128)S(1)}, f32[32]{0:T(128)S(1)}, u32[]{:S(2)}, u32[]{:S(2)}) %collective-permute-start.7) | collective-permute-done | bytes 160 | tf_op jit(solution)/shard_map/ppermute | solution.py:279
  60.7 2.9 %collective-permute-done.10 = f32[1,4]{1,0:T(1,128)S(1)} collective-permute-done((f32[1,4]{1,0:T(1,128)S(1)}, f32[1,4]{1,0:T(1,128)S(1)}, u32[]{:S(2)}, u32[]{:S(2)}) %collective-permute-start.10) | collective-permute-done | bytes 48 | tf_op jit(solution)/shard_map/ppermute | solution.py:279
  63.6 1.6 %collective-permute-start.11 = (f32[1,4]{1,0:T(1,128)S(1)}, f32[1,4]{1,0:T(1,128)S(1)}, u32[]{:S(2)}, u32[]{:S(2)}) collective-permute-start(f32[1,4]{1,0:T(1,128)S(1)} %get-tuple-element.50), channel_id=1, source_target_pairs={{0,24},{4,28},{8,16},{12,20},{16,8},{20,12},{24,0},{28,4},{1,25},{... | collective-permute-start | bytes 56 | tf_op jit(solution)/shard_map/ppermute | solution.py:279
  65.2 2.9 %collective-permute-done.11 = f32[1,4]{1,0:T(1,128)S(1)} collective-permute-done((f32[1,4]{1,0:T(1,128)S(1)}, f32[1,4]{1,0:T(1,128)S(1)}, u32[]{:S(2)}, u32[]{:S(2)}) %collective-permute-start.11) | collective-permute-done | bytes 48 | tf_op jit(solution)/shard_map/ppermute | solution.py:279
  68.1 1.5 %collective-permute-start.9 = (f32[1,4]{1,0:T(1,128)S(1)}, f32[1,4]{1,0:T(1,128)S(1)}, u32[]{:S(2)}, u32[]{:S(2)}) collective-permute-start(f32[1,4]{1,0:T(1,128)S(1)} %get-tuple-element.52), channel_id=1, source_target_pairs={{0,8},{4,12},{8,0},{12,4},{16,24},{20,28},{24,16},{28,20},{1,9},{5... | collective-permute-start | bytes 56 | tf_op jit(solution)/shard_map/ppermute | solution.py:279
  69.6 2.1 %collective-permute-done.9 = f32[1,4]{1,0:T(1,128)S(1)} collective-permute-done((f32[1,4]{1,0:T(1,128)S(1)}, f32[1,4]{1,0:T(1,128)S(1)}, u32[]{:S(2)}, u32[]{:S(2)}) %collective-permute-start.9) | collective-permute-done | bytes 48 | tf_op jit(solution)/shard_map/ppermute | solution.py:279
  71.7 1.5 %collective-permute-start.13 = (bf16[3,256,512]{2,1,0:T(8,128)(2,1)}, bf16[3,256,512]{2,1,0:T(8,128)(2,1)}, u32[]{:S(2)}, u32[]{:S(2)}) collective-permute-start(bf16[3,256,512]{2,1,0:T(8,128)(2,1)} %get-tuple-element.44), channel_id=1, source_target_pairs={{0,8},{4,12},{8,0},{12,4},{16,24},{20,28},{24,16},{28,20},{1,9},{5... | collective-permute-start | bytes 2359304 | tf_op jit(solution)/shard_map/ppermute | solution.py:279
  73.2 2.2 %copy-done = bf16[2048,1024]{1,0:T(8,128)(2,1)S(1)} copy-done((bf16[2048,1024]{1,0:T(8,128)(2,1)S(1)}, bf16[2048,1024]{1,0:T(8,128)(2,1)}, u32[]{:S(2)}) %copy-start) | copy-done | bytes 4194328
  76.4 2.0 %turn.2.lhs_ref = bf16[1024,1536]{1,0:T(8,128)(2,1)S(1)} custom-call(s32[6]{0:T(128)S(1)} %broadcast_xor_fusion.1.place, bf16[2048,1024]{1,0:T(8,128)(2,1)S(1)} %copy-done), custom_call_target="tpu_custom_call" | custom-call | flops 471859200 | bytes 6291456 | tf_op jit(solution)/shard_map/turn/pallas_call | solution.py:99
  78.4 1.3 constant_dynamic-slice_fusion
  81.7 10.8 %collective-permute-done.13.refs_4_ = bf16[3,256,512]{2,1,0:T(8,128)(2,1)} collective-permute-done((bf16[3,256,512]{2,1,0:T(8,128)(2,1)}, bf16[3,256,512]{2,1,0:T(8,128)(2,1)}, u32[]{:S(2)}, u32[]{:S(2)}) %collective-permute-start.13) | collective-permute-done | bytes 786464 | tf_op jit(solution)/shard_map/ppermute | solution.py:279
  92.4 1.6 %collective-permute-start.19 = (bf16[1,256,512]{2,1,0:T(8,128)(2,1)S(1)}, bf16[1,256,512]{2,1,0:T(8,128)(2,1)S(1)}, u32[]{:S(2)}, u32[]{:S(2)}) collective-permute-start(bf16[1,256,512]{2,1,0:T(8,128)(2,1)S(1)} %get-tuple-element.37), channel_id=1, source_target_pairs={{0,24},{4,28},{8,16},{12,20},{16,8},{20,12},{24,0},{28,4},{1,25},{... | collective-permute-start | bytes 786440 | tf_op jit(solution)/shard_map/ppermute | solution.py:279
  94.0 2.4 %collective-permute-start.20 = (bf16[1,256,512]{2,1,0:T(8,128)(2,1)S(1)}, bf16[1,256,512]{2,1,0:T(8,128)(2,1)S(1)}, u32[]{:S(2)}, u32[]{:S(2)}) collective-permute-start(bf16[1,256,512]{2,1,0:T(8,128)(2,1)S(1)} %get-tuple-element.36), channel_id=1, source_target_pairs={{0,28},{4,24},{8,20},{12,16},{16,12},{20,8},{24,4},{28,0},{1,29},{... | collective-permute-start | bytes 786440 | tf_op jit(solution)/shard_map/ppermute | solution.py:279
  96.4 1.3 collective-permute-start.17
  97.7 8.8 %near.1.near_ref = f32[4,1024,512]{2,1,0:T(8,128)S(1)} custom-call(bf16[1024,1536]{1,0:T(8,128)(2,1)S(1)} %turn.2.lhs_ref, bf16[4,256,512]{2,1,0:T(8,128)(2,1)S(1)} %get-tuple-element.43.refs_0_, bf16[1,256,512]{2,1,0:T(8,128)(2,1)S(1)} %copy-done.2, bf16[3,256,512]{2,1,0:T(8,128)(2,1)} %collective-permute-done.12.refs_2_, ...), custom_call_target="tpu_custom_call" | custom-call | flops 6442450944 | bytes 8388608 | tf_op jit(solution)/shard_map/near/pallas_call | solution.py:143
  106.5 20.9 %collective-permute-done.17.refs_0_ = bf16[1,256,512]{2,1,0:T(8,128)(2,1)S(1)} collective-permute-done((bf16[1,256,512]{2,1,0:T(8,128)(2,1)S(1)}, bf16[1,256,512]{2,1,0:T(8,128)(2,1)S(1)}, u32[]{:S(2)}, u32[]{:S(2)}) %collective-permute-start.17) | collective-permute-done | bytes 262176 | tf_op jit(solution)/shard_map/ppermute | solution.py:279
  127.9 2.0 %far.2.refs_2_ = bf16[4,1024,512]{2,1,0:T(8,128)(2,1)} custom-call(bf16[1024,512]{1,0:T(8,128)(2,1)S(1)} %turn.3.lhs_ref, f32[4,1024,512]{2,1,0:T(8,128)S(1)} %near.1.near_ref, bf16[2,256,512]{2,1,0:T(8,128)(2,1)S(1)} %collective-permute-done.21.refs_0_, bf16[2,256,512]{2,1,0:T(8,128)(2,1)S(1)} %collective-permute-done.22.refs_1_), custom_call_target="tpu_custom_call" | custom-call | flops 1073741824 | bytes 4194304 | tf_op jit(solution)/shard_map/far/pallas_call | solution.py:186
  129.9 1.5 %far.3._ = bf16[4,1024,512]{2,1,0:T(8,128)(2,1)} custom-call(bf16[1024,512]{1,0:T(8,128)(2,1)S(1)} %turn.3.lhs_ref, f32[4,1024,512]{2,1,0:T(8,128)S(1)} %near.1.near_ref, bf16[1,256,512]{2,1,0:T(8,128)(2,1)S(1)} %collective-permute-done.19.refs_0_, bf16[1,256,512]{2,1,0:T(8,128)(2,1)S(1)} %collective-permute-done.20.refs_1_, ...), custom_call_target="tpu_custom_call", output_to_operand_aliasing={{}: (4, {})} | custom-call | flops 536870912 | bytes 2097152 | tf_op jit(solution)/shard_map/far/pallas_call | solution.py:186
  131.9 4.9 %collective-permute-done.18.block_ref = bf16[1,256,512]{2,1,0:T(8,128)(2,1)S(1)} collective-permute-done((bf16[1,256,512]{2,1,0:T(8,128)(2,1)S(1)}, bf16[1,256,512]{2,1,0:T(8,128)(2,1)S(1)}, u32[]{:S(2)}, u32[]{:S(2)}) %collective-permute-start.18) | collective-permute-done | bytes 262176 | tf_op jit(solution)/shard_map/ppermute | solution.py:279
  (57 shorter events, 13.6 us)
Async XLA Ops:
  1.7 9.8 %collective-permute-start = (bf16[1,256,512]{2,1,0:T(8,128)(2,1)S(1)}, bf16[1,256,512]{2,1,0:T(8,128)(2,1)S(1)}, u32[]{:S(2)}, u32[]{:S(2)}) collective-permute-start(bf16[1,256,512]{2,1,0:T(8,128)(2,1)S(1)} %get-tuple-element.18), channel_id=1, source_target_pairs={{0,16},{4,20},{8,24},{12,28},{16,0},{20,4},{24,8},{28,12},{1,17},{... | collective-permute-start | bytes 786440 | tf_op jit(solution)/shard_map/ppermute | solution.py:279
  4.8 7.8 %collective-permute-start.1 = (bf16[1,256,512]{2,1,0:T(8,128)(2,1)S(1)}, bf16[1,256,512]{2,1,0:T(8,128)(2,1)S(1)}, u32[]{:S(2)}, u32[]{:S(2)}) collective-permute-start(bf16[1,256,512]{2,1,0:T(8,128)(2,1)S(1)} %get-tuple-element.19), channel_id=1, source_target_pairs={{0,8},{4,12},{8,0},{12,4},{16,24},{20,28},{24,16},{28,20},{1,9},{5... | collective-permute-start | bytes 786440 | tf_op jit(solution)/shard_map/ppermute | solution.py:279
  9.0 72.0 %collective-permute-start.12 = (bf16[3,256,512]{2,1,0:T(8,128)(2,1)}, bf16[3,256,512]{2,1,0:T(8,128)(2,1)}, u32[]{:S(2)}, u32[]{:S(2)}) collective-permute-start(bf16[3,256,512]{2,1,0:T(8,128)(2,1)} %get-tuple-element.45), channel_id=1, source_target_pairs={{0,16},{4,20},{8,24},{12,28},{16,0},{20,4},{24,8},{28,12},{1,17},{... | collective-permute-start | bytes 2359304 | tf_op jit(solution)/shard_map/ppermute | solution.py:279
  11.4 5.7 %copy-start.1 = (bf16[1,256,512]{2,1,0:T(8,128)(2,1)}, bf16[1,256,512]{2,1,0:T(8,128)(2,1)S(1)}, u32[]{:S(2)}) copy-start(bf16[1,256,512]{2,1,0:T(8,128)(2,1)S(1)} %collective-permute-done.refs_1_) | copy-start | bytes 786436
  12.5 4.6 %copy-start.3 = (bf16[1,256,512]{2,1,0:T(8,128)(2,1)}, bf16[1,256,512]{2,1,0:T(8,128)(2,1)S(1)}, u32[]{:S(2)}) copy-start(bf16[1,256,512]{2,1,0:T(8,128)(2,1)S(1)} %collective-permute-done.1.refs_3_) | copy-start | bytes 786436
  17.1 11.4 %collective-permute-start.2 = (bf16[256,512]{1,0:T(8,128)(2,1)}, bf16[256,512]{1,0:T(8,128)(2,1)S(1)}, u32[]{:S(2)}, u32[]{:S(2)}) collective-permute-start(bf16[256,512]{1,0:T(8,128)(2,1)} %get-tuple-element.48), channel_id=1, source_target_pairs={{0,1},{1,0},{2,3},{3,2},{4,5},{5,4},{6,7},{7,6},{8,9},{9,8},{10,11... | collective-permute-start | bytes 786440 | tf_op jit(solution)/shard_map/ppermute | solution.py:279
  18.7 21.5 %collective-permute-start.3 = (bf16[256,512]{1,0:T(8,128)(2,1)}, bf16[256,512]{1,0:T(8,128)(2,1)S(1)}, u32[]{:S(2)}, u32[]{:S(2)}) collective-permute-start(bf16[256,512]{1,0:T(8,128)(2,1)} %get-tuple-element.47), channel_id=1, source_target_pairs={{0,2},{1,3},{2,0},{3,1},{4,6},{5,7},{6,4},{7,5},{8,10},{9,11},{10,... | collective-permute-start | bytes 786440 | tf_op jit(solution)/shard_map/ppermute | solution.py:279
  21.3 18.9 %collective-permute-start.4 = (bf16[256,512]{1,0:T(8,128)(2,1)S(1)}, bf16[256,512]{1,0:T(8,128)(2,1)S(1)}, u32[]{:S(2)}, u32[]{:S(2)}) collective-permute-start(bf16[256,512]{1,0:T(8,128)(2,1)S(1)} %get-tuple-element.46), channel_id=1, source_target_pairs={{0,3},{1,2},{2,1},{3,0},{4,7},{5,6},{6,5},{7,4},{8,11},{9,10},{10,... | collective-permute-start | bytes 786440 | tf_op jit(solution)/shard_map/ppermute | solution.py:279
  25.5 66.9 %collective-permute-start.14 = (bf16[4,256,512]{2,1,0:T(8,128)(2,1)}, bf16[4,256,512]{2,1,0:T(8,128)(2,1)S(1)}, u32[]{:S(2)}, u32[]{:S(2)}) collective-permute-start(bf16[4,256,512]{2,1,0:T(8,128)(2,1)} %get-tuple-element.42), channel_id=1, source_target_pairs={{0,20},{4,16},{8,28},{12,24},{16,4},{20,0},{24,12},{28,8},{1,21},{... | collective-permute-start | bytes 3145736 | tf_op jit(solution)/shard_map/ppermute | solution.py:279
  28.5 44.7 %copy-start.7 = (s32[6]{0:T(128)S(1)}, s32[6]{0:T(128)}, u32[]{:S(2)}) copy-start(s32[6]{0:T(128)} %constant.48.clone) | copy-start | bytes 76
  28.5 44.7 %copy-start.6 = (s32[2]{0:T(128)S(1)}, s32[2]{0:T(128)}, u32[]{:S(2)}) copy-start(s32[2]{0:T(128)} %constant.49.clone) | copy-start | bytes 28
  28.5 65.5 %collective-permute-start.15 = (bf16[4,256,512]{2,1,0:T(8,128)(2,1)}, bf16[4,256,512]{2,1,0:T(8,128)(2,1)}, u32[]{:S(2)}, u32[]{:S(2)}) collective-permute-start(bf16[4,256,512]{2,1,0:T(8,128)(2,1)} %get-tuple-element.41), channel_id=1, source_target_pairs={{0,12},{4,8},{8,4},{12,0},{16,28},{20,24},{24,20},{28,16},{1,13},{... | collective-permute-start | bytes 3145736 | tf_op jit(solution)/shard_map/ppermute | solution.py:279
  48.0 5.3 %collective-permute-start.5 = (f32[32]{0:T(128)S(1)}, f32[32]{0:T(128)S(1)}, u32[]{:S(2)}, u32[]{:S(2)}) collective-permute-start(f32[32]{0:T(128)S(1)} %get-tuple-element.55), channel_id=1, source_target_pairs={{0,1},{1,0},{2,3},{3,2},{4,5},{5,4},{6,7},{7,6},{8,9},{9,8},{10,11... | collective-permute-start | bytes 392 | tf_op jit(solution)/shard_map/ppermute | solution.py:279
  51.8 4.5 %collective-permute-start.6 = (f32[32]{0:T(128)S(1)}, f32[32]{0:T(128)S(1)}, u32[]{:S(2)}, u32[]{:S(2)}) collective-permute-start(f32[32]{0:T(128)S(1)} %get-tuple-element.53), channel_id=1, source_target_pairs={{0,2},{1,3},{2,0},{3,1},{4,6},{5,7},{6,4},{7,5},{8,10},{9,11},{10,... | collective-permute-start | bytes 392 | tf_op jit(solution)/shard_map/ppermute | solution.py:279
  53.3 5.4 %collective-permute-start.7 = (f32[32]{0:T(128)S(1)}, f32[32]{0:T(128)S(1)}, u32[]{:S(2)}, u32[]{:S(2)}) collective-permute-start(f32[32]{0:T(128)S(1)} %get-tuple-element.54), channel_id=1, source_target_pairs={{0,3},{1,2},{2,1},{3,0},{4,7},{5,6},{6,5},{7,4},{8,11},{9,10},{10,... | collective-permute-start | bytes 392 | tf_op jit(solution)/shard_map/ppermute | solution.py:279
  56.2 40.1 %collective-permute-start.16 = (bf16[4,256,512]{2,1,0:T(8,128)(2,1)}, bf16[4,256,512]{2,1,0:T(8,128)(2,1)S(1)}, u32[]{:S(2)}, u32[]{:S(2)}) collective-permute-start(bf16[4,256,512]{2,1,0:T(8,128)(2,1)} %get-tuple-element.40), channel_id=1, source_target_pairs={{0,4},{4,0},{8,12},{12,8},{16,20},{20,16},{24,28},{28,24},{1,5},{5... | collective-permute-start | bytes 3145736 | tf_op jit(solution)/shard_map/ppermute | solution.py:279
  58.8 1.2 collective-permute-start.8
  60.0 3.6 %collective-permute-start.10 = (f32[1,4]{1,0:T(1,128)S(1)}, f32[1,4]{1,0:T(1,128)S(1)}, u32[]{:S(2)}, u32[]{:S(2)}) collective-permute-start(f32[1,4]{1,0:T(1,128)S(1)} %get-tuple-element.51), channel_id=1, source_target_pairs={{0,16},{4,20},{8,24},{12,28},{16,0},{20,4},{24,8},{28,12},{1,17},{... | collective-permute-start | bytes 56 | tf_op jit(solution)/shard_map/ppermute | solution.py:279
  63.6 4.5 %collective-permute-start.11 = (f32[1,4]{1,0:T(1,128)S(1)}, f32[1,4]{1,0:T(1,128)S(1)}, u32[]{:S(2)}, u32[]{:S(2)}) collective-permute-start(f32[1,4]{1,0:T(1,128)S(1)} %get-tuple-element.50), channel_id=1, source_target_pairs={{0,24},{4,28},{8,16},{12,20},{16,8},{20,12},{24,0},{28,4},{1,25},{... | collective-permute-start | bytes 56 | tf_op jit(solution)/shard_map/ppermute | solution.py:279
  68.1 3.6 %collective-permute-start.9 = (f32[1,4]{1,0:T(1,128)S(1)}, f32[1,4]{1,0:T(1,128)S(1)}, u32[]{:S(2)}, u32[]{:S(2)}) collective-permute-start(f32[1,4]{1,0:T(1,128)S(1)} %get-tuple-element.52), channel_id=1, source_target_pairs={{0,8},{4,12},{8,0},{12,4},{16,24},{20,28},{24,16},{28,20},{1,9},{5... | collective-permute-start | bytes 56 | tf_op jit(solution)/shard_map/ppermute | solution.py:279
  71.7 20.7 %collective-permute-start.13 = (bf16[3,256,512]{2,1,0:T(8,128)(2,1)}, bf16[3,256,512]{2,1,0:T(8,128)(2,1)}, u32[]{:S(2)}, u32[]{:S(2)}) collective-permute-start(bf16[3,256,512]{2,1,0:T(8,128)(2,1)} %get-tuple-element.44), channel_id=1, source_target_pairs={{0,8},{4,12},{8,0},{12,4},{16,24},{20,28},{24,16},{28,20},{1,9},{5... | collective-permute-start | bytes 2359304 | tf_op jit(solution)/shard_map/ppermute | solution.py:279
  73.2 2.2 %copy-start = (bf16[2048,1024]{1,0:T(8,128)(2,1)S(1)}, bf16[2048,1024]{1,0:T(8,128)(2,1)}, u32[]{:S(2)}) copy-start(bf16[2048,1024]{1,0:T(8,128)(2,1)} %source_ref.1) | copy-start | bytes 12582916
  76.4 21.3 %copy-start.2 = (bf16[1,256,512]{2,1,0:T(8,128)(2,1)S(1)}, bf16[1,256,512]{2,1,0:T(8,128)(2,1)}, u32[]{:S(2)}) copy-start(bf16[1,256,512]{2,1,0:T(8,128)(2,1)} %copy-done.1) | copy-start | bytes 786436
  76.4 21.3 %copy-start.4 = (bf16[1,256,512]{2,1,0:T(8,128)(2,1)S(1)}, bf16[1,256,512]{2,1,0:T(8,128)(2,1)}, u32[]{:S(2)}) copy-start(bf16[1,256,512]{2,1,0:T(8,128)(2,1)} %copy-done.3) | copy-start | bytes 786436
  81.0 46.9 %collective-permute-start.21 = (bf16[2,256,512]{2,1,0:T(8,128)(2,1)S(1)}, bf16[2,256,512]{2,1,0:T(8,128)(2,1)S(1)}, u32[]{:S(2)}, u32[]{:S(2)}) collective-permute-start(bf16[2,256,512]{2,1,0:T(8,128)(2,1)S(1)} %get-tuple-element.35), channel_id=1, source_target_pairs={{0,24},{4,28},{8,16},{12,20},{16,8},{20,12},{24,0},{28,4},{1,25},{... | collective-permute-start | bytes 1572872 | tf_op jit(solution)/shard_map/ppermute | solution.py:279
  92.4 35.5 %collective-permute-start.22 = (bf16[2,256,512]{2,1,0:T(8,128)(2,1)S(1)}, bf16[2,256,512]{2,1,0:T(8,128)(2,1)S(1)}, u32[]{:S(2)}, u32[]{:S(2)}) collective-permute-start(bf16[2,256,512]{2,1,0:T(8,128)(2,1)S(1)} %get-tuple-element.34), channel_id=1, source_target_pairs={{0,28},{4,24},{8,20},{12,16},{16,12},{20,8},{24,4},{28,0},{1,29},{... | collective-permute-start | bytes 1572872 | tf_op jit(solution)/shard_map/ppermute | solution.py:279
  92.4 37.5 %collective-permute-start.19 = (bf16[1,256,512]{2,1,0:T(8,128)(2,1)S(1)}, bf16[1,256,512]{2,1,0:T(8,128)(2,1)S(1)}, u32[]{:S(2)}, u32[]{:S(2)}) collective-permute-start(bf16[1,256,512]{2,1,0:T(8,128)(2,1)S(1)} %get-tuple-element.37), channel_id=1, source_target_pairs={{0,24},{4,28},{8,16},{12,20},{16,8},{20,12},{24,0},{28,4},{1,25},{... | collective-permute-start | bytes 786440 | tf_op jit(solution)/shard_map/ppermute | solution.py:279
  94.0 35.9 %collective-permute-start.20 = (bf16[1,256,512]{2,1,0:T(8,128)(2,1)S(1)}, bf16[1,256,512]{2,1,0:T(8,128)(2,1)S(1)}, u32[]{:S(2)}, u32[]{:S(2)}) collective-permute-start(bf16[1,256,512]{2,1,0:T(8,128)(2,1)S(1)} %get-tuple-element.36), channel_id=1, source_target_pairs={{0,28},{4,24},{8,20},{12,16},{16,12},{20,8},{24,4},{28,0},{1,29},{... | collective-permute-start | bytes 786440 | tf_op jit(solution)/shard_map/ppermute | solution.py:279
  96.4 31.0 %collective-permute-start.17 = (bf16[1,256,512]{2,1,0:T(8,128)(2,1)S(1)}, bf16[1,256,512]{2,1,0:T(8,128)(2,1)S(1)}, u32[]{:S(2)}, u32[]{:S(2)}) collective-permute-start(bf16[1,256,512]{2,1,0:T(8,128)(2,1)S(1)} %get-tuple-element.39), channel_id=1, source_target_pairs={{0,24},{4,28},{8,16},{12,20},{16,8},{20,12},{24,0},{28,4},{1,25},{... | collective-permute-start | bytes 786440 | tf_op jit(solution)/shard_map/ppermute | solution.py:279
  127.4 9.5 %collective-permute-start.18 = (bf16[1,256,512]{2,1,0:T(8,128)(2,1)S(1)}, bf16[1,256,512]{2,1,0:T(8,128)(2,1)S(1)}, u32[]{:S(2)}, u32[]{:S(2)}) collective-permute-start(bf16[1,256,512]{2,1,0:T(8,128)(2,1)S(1)} %get-tuple-element.38), channel_id=1, source_target_pairs={{0,28},{4,24},{8,20},{12,16},{16,12},{20,8},{24,4},{28,0},{1,29},{... | collective-permute-start | bytes 786440 | tf_op jit(solution)/shard_map/ppermute | solution.py:279
  129.9 1.5 %copy-start.5 = (f32[4]{0:T(128)S(1)}, f32[4]{0:T(128)}, u32[]{:S(2)}) copy-start(f32[4]{0:T(128)} %param.9) | copy-start | bytes 52
